TPU v7x, 256 devices: a whole 4x4x8 slice. The times are simulated.
256 devices in a mesh: rep: 2 (over core), dp: 128 (over x, y, z).
Axes of the slice: x: 4, y: 4, z: 8, core: 2. Of those that a mesh axis runs over, the one named last changes fastest.
Arguments:
- x: bfloat16 [256, 2048, 512], P(('rep', 'dp')), parts along dimension 0
- dy: bfloat16 [256, 2048, 512], P(('rep', 'dp')), parts along dimension 0
- w_gate: bfloat16 [2, 512, 3072], replicated
- w_up: bfloat16 [2, 512, 3072], replicated
- w_down: bfloat16 [2, 3072, 512], replicated
- m_w_gate: float32 [2, 512, 3072], P(None, 'dp')
- m_w_up: float32 [2, 512, 3072], P(None, 'dp')
- m_w_down: float32 [2, 3072, 512], P(None, 'dp')
- v_w_gate: float32 [2, 512, 3072], P(None, 'dp')
- v_w_up: float32 [2, 512, 3072], P(None, 'dp')
- v_w_down: float32 [2, 3072, 512], P(None, 'dp')
Outputs:
- output 1: bfloat16 [4, 512, 3072], P('rep'), parts along dimension 0
- output 2: bfloat16 [4, 512, 3072], P('rep'), parts along dimension 0
- output 3: bfloat16 [4, 3072, 512], P('rep'), parts along dimension 0
- output 4: float32 [4, 512, 3072], P('rep', 'dp'), parts along dimension 0
- output 5: float32 [4, 512, 3072], P('rep', 'dp'), parts along dimension 0
- output 6: float32 [4, 3072, 512], P('rep', 'dp'), parts along dimension 0
- output 7: float32 [4, 512, 3072], P('rep', 'dp'), parts along dimension 0
- output 8: float32 [4, 512, 3072], P('rep', 'dp'), parts along dimension 0
- output 9: float32 [4, 3072, 512], P('rep', 'dp'), parts along dimension 0
There are 2 independent parts. A program takes and returns all parts, laid end to end along the dimension named above; an argument that names none is the same for every part.
All inputs are finite; a program needn't handle non-finite values.
Results may differ from a plain program's by a relative error of at most 0.022.
Values are sent between devices in bfloat16 or wider.
A program may use at most 768 MiB of HBM per device.

v0:
```python
import jax
import jax.numpy as jnp
from jax import lax

NAMES = ("w_gate", "w_up", "w_down")


def matmul(a, w):
    return jnp.dot(a, w, preferred_element_type=jnp.float32).astype(jnp.bfloat16)


def normed(h):
    wide = h.astype(jnp.float32)
    scale = lax.rsqrt(jnp.mean(wide**2, -1, keepdims=True) + 1e-6)
    return (wide * scale).astype(jnp.bfloat16)


def layer(h, w):
    a = normed(h)
    gate = jnp.dot(a, w["w_gate"], preferred_element_type=jnp.float32)
    up = jnp.dot(a, w["w_up"], preferred_element_type=jnp.float32)
    return h + matmul((jax.nn.silu(gate) * up).astype(jnp.bfloat16), w["w_down"])


def adamw(w, m, v, g):
    m = 0.9 * m + 0.1 * g
    v = 0.95 * v + 0.05 * g * g
    step = m * lax.rsqrt(v + 1e-8) + 0.1 * w
    return (w - 0.02 * step).astype(jnp.bfloat16), m, v


def stack(weights, h):
    for number in range(weights["w_gate"].shape[0]):
        h = layer(h, {name: w[number] for name, w in weights.items()})
    return h


def solution(mesh):
    groups = mesh.shape["rep"]

    def step(x, dy, *arrays):
        weights, m, v = (arrays[i : i + 3] for i in (0, 3, 6))
        x, dy = (t.reshape(groups, -1, *t.shape[1:]) for t in (x, dy))

        def of_a_group(x, dy):
            _, back = jax.vjp(lambda w: stack(w, x), dict(zip(NAMES, weights, strict=True)))
            by_weights = back(dy)[0]
            gradients = [by_weights[name].astype(jnp.float32) for name in NAMES]
            new = [adamw(w.astype(jnp.float32), m, v, g) for w, m, v, g in zip(weights, m, v, gradients, strict=True)]
            return tuple(one[which] for which in range(3) for one in new)

        return tuple(t.reshape(-1, *t.shape[2:]) for t in jax.vmap(of_a_group)(x, dy))

    return step
```

profile of v0, /device:TPU:2, one launch (start us, length us, event | category | flops | bytes accessed | tf_op | source)
XLA Modules:
  0.0 2244.9 jit_solution(9572168065976859043)
XLA Ops:
  7.2 0.0 copy-start.1
  7.2 0.0 reduce-scatter.17.cloned.1.call-start
  7.2 2.2 fusion.47
  9.4 3.9 copy.2
  13.4 0.0 copy-start.17
  13.4 13.6 fusion.67
  27.0 13.6 fusion.65
  40.6 21.8 fusion.26
  62.4 10.8 fusion.51
  73.3 0.0 copy-start.15
  73.3 0.0 slice-start
  73.3 14.7 fusion.56
  88.0 13.9 fusion.59
  101.9 9.8 convolution_convert_fusion.1
  111.7 2.9 copy.3
  114.7 21.6 fusion.6
  136.2 4.5 copy-done
  140.8 9.3 fusion.80
  150.1 20.9 fusion.53
  171.0 3.6 fusion.108
  174.6 0.0 copy-start.8
  174.6 1.3 copy-done.8
  175.9 11.7 convolution_bitcast_fusion
  187.7 0.0 reduce-scatter.17.cloned.1.call-update
  187.7 0.0 reduce-scatter.15.cloned.1.call-start
  187.7 1.5 copy-done.3
  189.3 20.8 fusion.35
  210.0 0.0 reduce-scatter.15.cloned.1.call-update
  210.0 0.0 copy-start.5
  210.1 0.0 copy-start.18
  210.1 0.0 all-gather.12.cloned.1.call-start
  210.1 11.9 convolution_convert_fusion
  222.0 18.2 fusion.44
  240.2 25.3 %fusion.38 = f32[1,512,3072]{2,1,0:T(8,128)} fusion(f32[2048,3072]{1,0:T(8,128)} %fusion.67, f32[2048,3072]{1,0:T(8,128)} %fusion.65, bf16[2048,3072]{1,0:T(8,128)(2,1)} %convolution_convert_fusion, bf16[1,2048,512]{1,2,0:T(8,128)(2,1)S(1)} %copy-done.5, f32[2048]{0:T(1024)S(1)} %copy-done.18), kind=kOutput, calls=%fused_computation.53 | convolution fusion | flops 6514802688 | bytes 71311360 | tf_op jit(solution)/vmap(transpose(jvp()))/dot_general | solution.py:20
  265.5 13.8 convolution_bitcast_fusion.1
  279.3 0.6 fusion.156
  280.5 18.1 fusion.41
  299.3 0.0 copy-start.9
  299.3 0.0 copy-start.10
  299.4 0.0 copy-start.12
  299.4 0.0 copy-start.13
  299.4 776.5 %all-reduce.12 = (bf16[1,512,3072]{2,1,0:T(8,128)(2,1)}, bf16[1,512,3072]{2,1,0:T(8,128)(2,1)}, bf16[1,512,3072]{2,1,0:T(8,128)(2,1)}, bf16[1,512,3072]{2,1,0:T(8,128)(2,1)}) all-reduce(f32[1,512,3072]{2,1,0:T(8,128)} %fusion.38, f32[1,512,3072]{2,1,0:T(8,128)} %convolution_bitcast_fusion.1, ...), channel_id=14, replica_groups=[2,128]<=[256], use_global_device_ids=true, to_apply=%add.1.clone.clone | all-reduce | flops 6291456 | bytes 37748736
  1075.9 0.8 fusion.149
  1076.8 1.7 fusion.145
  1078.5 0.7 copy.5
  1079.1 0.0 all-gather.12.cloned.1.call-update
  1079.1 0.0 all-gather.10.cloned.1.call-start
  1079.2 0.9 fusion.147
  1080.1 1.7 fusion.146
  1081.8 0.7 copy.4
  1082.4 0.0 all-gather.10.cloned.1.call-update
  1082.5 0.0 all-gather.14.cloned.1.call-start
  1082.5 0.0 reduce-scatter.17.cloned.1.call-done
  1082.5 0.8 convert_bitcast_fusion.3
  1083.3 786.5 %reduce-scatter.15.cloned.1.call-done = f32[1,24,512]{2,1,0:T(8,128)} async-done(((f32[1,3072,512]{2,1,0:T(8,128)}), f32[1,24,512]{2,1,0:T(8,128)}) %reduce-scatter.15.cloned.1.call-update) | async-done | bytes 49168
  1869.8 0.8 convert_bitcast_fusion.4
  1870.6 1.5 fusion.142
  1872.2 0.0 all-gather.14.cloned.1.call-update
  1872.2 119.7 %all-gather.12.cloned.1.call-done = bf16[1,2,512,3072]{3,1,0,2:T(2,128)(2,1)} async-done(((bf16[1,2,4,3072]{3,1,0,2:T(2,128)(2,1)}), bf16[1,2,512,3072]{3,1,0,2:T(2,128)(2,1)}) %all-gather.12.cloned.1.call-update) | async-done | bytes 6291472 | tf_op jit(solution)/reshape | solution.py:52
  1991.9 7.3 copy.7
  1999.2 113.0 %all-gather.10.cloned.1.call-done = bf16[1,2,512,3072]{3,1,0,2:T(2,128)(2,1)} async-done(((bf16[1,2,4,3072]{3,1,0,2:T(2,128)(2,1)}), bf16[1,2,512,3072]{3,1,0,2:T(2,128)(2,1)}) %all-gather.10.cloned.1.call-update) | async-done | bytes 6291472 | tf_op jit(solution)/reshape | solution.py:52
  2112.2 7.3 copy.6
  2119.5 112.5 %all-gather.14.cloned.1.call-done = bf16[1,2,3072,512]{3,2,1,0:T(8,128)(2,1)} async-done(((bf16[1,2,24,512]{3,2,1,0:T(8,128)(2,1)}), bf16[1,2,3072,512]{3,2,1,0:T(8,128)(2,1)}) %all-gather.14.cloned.1.call-update) | async-done | bytes 6291472 | tf_op jit(solution)/reshape | solution.py:52
  2232.1 5.9 copy.25
  (35 shorter events, 0.1 us)
Async XLA Ops:
  7.2 6.2 copy-start.1
  7.2 1075.3 %reduce-scatter.17.cloned.1.call-start = ((), (), s32[]{:S(2)}) async-start(), calls=%async_computation.6 | async-start | bytes 6340608
  13.4 13.6 copy-start.17
  40.6 21.8 copy-start.4
  73.2 14.8 copy-start.6
  73.3 97.8 %copy-start.15 = (f32[1,1,2048]{2,1,0:T(1,128)}, f32[1,1,2048]{2,1,0:T(1,128)S(1)}, u32[]{:S(2)}) copy-start(f32[1,1,2048]{2,1,0:T(1,128)S(1)} %rsqrt.31) | copy-start | bytes 24580
  73.3 28.6 %slice-start = ((s8[6291456]{0:T(1024)(128)(4,1)}), s8[4194304]{0:T(1024)(128)(4,1)S(1)}, s32[]{:S(2)}) async-start(s8[6291456]{0:T(1024)(128)(4,1)} %bitcast.385), calls=%async_computation.7 | async-start | bytes 8388608
  88.0 13.9 copy-start.2
  88.0 13.9 slice-start.1
  136.2 4.6 copy-start
  174.6 1.3 copy-start.8
  187.7 1.6 copy-start.3
  187.7 1682.1 %reduce-scatter.15.cloned.1.call-start = ((), (), s32[]{:S(2)}) async-start(), calls=%async_computation.5 | async-start | bytes 6340608
  210.0 12.0 copy-start.5
  210.1 12.0 copy-start.18
  210.1 1781.8 %all-gather.12.cloned.1.call-start = ((), (), s32[]{:S(2)}) async-start(), calls=%async_computation.3 | async-start | bytes 6340608 | tf_op jit(solution)/reshape | solution.py:52
  240.2 25.3 %copy-start.16 = (f32[1,1,2048]{2,1,0:T(1,128)S(1)}, f32[1,1,2048]{2,1,0:T(1,128)}, u32[]{:S(2)}) copy-start(f32[1,1,2048]{2,1,0:T(1,128)} %copy-done.15) | copy-start | bytes 24580
  265.5 13.8 copy-start.19
  265.5 15.0 copy-start.7
  299.3 777.4 %copy-start.9 = (f32[2,4,3072]{2,1,0:T(4,128)S(1)}, f32[2,4,3072]{2,1,0:T(4,128)}, u32[]{:S(2)}) copy-start(f32[2,4,3072]{2,1,0:T(4,128)} %param.8) | copy-start | bytes 294916
  299.3 777.4 %copy-start.10 = (f32[2,4,3072]{2,1,0:T(4,128)S(1)}, f32[2,4,3072]{2,1,0:T(4,128)}, u32[]{:S(2)}) copy-start(f32[2,4,3072]{2,1,0:T(4,128)} %param.7) | copy-start | bytes 294916
  299.4 780.7 %copy-start.11 = (f32[2,4,3072]{2,1,0:T(4,128)S(1)}, f32[2,4,3072]{2,1,0:T(4,128)}, u32[]{:S(2)}) copy-start(f32[2,4,3072]{2,1,0:T(4,128)} %param.6) | copy-start | bytes 294916
  299.4 780.7 %copy-start.12 = (f32[2,4,3072]{2,1,0:T(4,128)S(1)}, f32[2,4,3072]{2,1,0:T(4,128)}, u32[]{:S(2)}) copy-start(f32[2,4,3072]{2,1,0:T(4,128)} %param.1) | copy-start | bytes 294916
  299.4 1571.2 %copy-start.13 = (f32[2,24,512]{2,1,0:T(8,128)S(1)}, f32[2,24,512]{2,1,0:T(8,128)}, u32[]{:S(2)}) copy-start(f32[2,24,512]{2,1,0:T(8,128)} %param.10) | copy-start | bytes 294916
  299.4 1571.2 %copy-start.14 = (f32[2,24,512]{2,1,0:T(8,128)S(1)}, f32[2,24,512]{2,1,0:T(8,128)}, u32[]{:S(2)}) copy-start(f32[2,24,512]{2,1,0:T(8,128)} %param.9) | copy-start | bytes 294916
  1079.1 1033.1 %all-gather.10.cloned.1.call-start = ((), (), s32[]{:S(2)}) async-start(), calls=%async_computation.2 | async-start | bytes 6340608 | tf_op jit(solution)/reshape | solution.py:52
  1082.5 1149.6 %all-gather.14.cloned.1.call-start = ((), (), s32[]{:S(2)}) async-start(), calls=%async_computation.4 | async-start | bytes 6340608 | tf_op jit(solution)/reshape | solution.py:52
Sparse Core Ops, SparseCore 0:
  187.8 854.8 reduce-scatter.16
  1048.3 821.4 reduce-scatter.14
  1874.0 117.7 all-gather.11
  1996.0 116.2 all-gather.9
  2115.8 116.2 all-gather.13
where the time goes:
time: 2250 us; the launch traced here: 2240 us
  waiting for transfers between devices  1130 us (50%)
  blocking collectives  776 us (34%)
  matrix products  226 us (10%)
  other arithmetic  55.7 us (2%)
  local copies, waits for them, and re-layouts  38.5 us (2%)
    unnamed x7, waiting for transfers between devices  787 us
    unnamed x1, blocking collectives  776 us
    reshape x3, waiting for transfers between devices, step(): t.reshape(-1, *t.shape[2:])  345 us
    dot_general x5, matrix products, layer(): up = jnp.dot(a, w['w_up'], preferred_element_type=jnp.float32)  84.7 us
    dot_general x5, matrix products, layer(): gate = jnp.dot(a, w['w_gate'], preferred_element_type=jnp.float32)  76.7 us
    dot_general x5, matrix products, matmul(): jnp.dot(a, w, preferred_element_type=jnp.float32).astype(jnp.bfloat16)  65 us
    unnamed x4, other arithmetic  46.9 us
  transfers between devices with their start and end apart: 5, of which 4 were waited for; matrix products, arithmetic and copies ran while one was open for 6% of the time, Pallas kernels for 0%

commit v1 on v0

v1 whole, which is shorter than its diff:
```python
import jax
import jax.numpy as jnp
from jax import lax
from jax.experimental import pallas as pl
from jax.experimental.pallas import tpu as pltpu
from jax.sharding import PartitionSpec as P

MESH = pl.DeviceIdType.MESH
F32, BF16 = jnp.float32, jnp.bfloat16
TOK, D, FF = 2048, 512, 3072
CW = 768
HW = CW // 2
HF = FF // 2
HD = D // 2
LN = 128
CHUNKS = FF // CW
LAST = 2 * CHUNKS
PAIR = (0, 1)
FOUR = range(4)
EIGHT = range(8)
T = 512
SUB = 256


def f32(v):
    return v.astype(F32)


def b16(v):
    return v.astype(BF16)


def dot(a, b):
    return jnp.dot(a, b, preferred_element_type=F32)


def dot_t(a, b):
    return lax.dot_general(a, b, (((1,), (1,)), ((), ())), preferred_element_type=F32)


def rows_of(t, n):
    return pl.ds(pl.multiple_of(t * n, n), n)


def part(i, n):
    return pl.ds(i * n, n)


def flip(p):
    return p + 1 - 2 * lax.rem(p, 2)


def mirror(p):
    return 3 - p


def partners(p, half):
    return (mirror(p), flip(p)) if half else (flip(p), mirror(p))


def passed(p, half):
    first, _ = partners(p, half)
    return first, partners(first, half)[1]


def kept(p, half):
    return p, partners(p, half)[1]


def layer_of(c):
    return jnp.where(c < CHUNKS, 1, 0)


def go(copies):
    for c in copies:
        c.start()


def arrive(copies):
    for c in copies:
        c.wait_recv()


def leave(copies):
    for c in copies:
        c.wait_send()


def adamw(w, m, v, g):
    m = 0.9 * m + 0.1 * g
    v = 0.95 * v + 0.05 * g * g
    step = m * lax.rsqrt(v + 1e-8) + 0.1 * w
    return b16(w - 0.02 * step), m, v


COUNTS = dict(c1=8, c2=4, c3=4, c4=4, cf=7, a0=7, a1=4, a2=8, a3=4, a4=8, ring=14, dy1=2, dy2=2, dx=3, ex=3, ey1=2, ey2=4, back=14)
FIRST = {}
SEMS = 0
for _name, _n in COUNTS.items():
    FIRST[_name] = SEMS
    SEMS += 2 * _n


class Step:
    def __init__(self, refs):
        self.__dict__.update(refs)
        d = lax.axis_index("dp")
        self.rep = lax.axis_index("rep")
        self.x, self.y, self.z = d // 32, lax.rem(d // 8, 4), lax.rem(d, 8)


    def at(self, x=None, y=None, z=None):
        x = self.x if x is None else x
        y = self.y if y is None else y
        z = self.z if z is None else z
        return (self.rep, x * 32 + y * 8 + z)

    def up_z(self, i):
        return lax.rem(self.z + i + 16, 8)

    def up_x(self, i):
        return lax.rem(self.x + i + 4, 4)

    def copy(self, sem, src, dst, dev):
        return pltpu.make_async_remote_copy(
            src_ref=src, dst_ref=dst, send_sem=self.ssem.at[sem], recv_sem=self.rsem.at[sem], device_id=dev, device_id_type=MESH
        )

    def copies(self, name, c, moves):
        base = FIRST[name] + lax.rem(c, 2) * COUNTS[name]
        return [self.copy(base + i, *move) for i, move in enumerate(moves)]

    def barrier(self):
        b = pltpu.get_barrier_semaphore()
        to = [self.at(z=self.up_z(i)) for i in range(1, 8)] + [self.at(x=self.up_x(i)) for i in range(1, 4)]
        to += [self.at(y=flip(self.y)), self.at(y=mirror(self.y))]
        for q in to:
            pl.semaphore_signal(b, inc=1, device_id=q, device_id_type=MESH)
        pl.semaphore_wait(b, len(to))


    def outer(self, w):
        return self.y if w else self.x

    def inner(self, w):
        return self.x if w else self.y

    def at_outer(self, w, p):
        return self.at(y=p) if w else self.at(x=p)

    def at_inner(self, w, p):
        return self.at(x=p) if w else self.at(y=p)

    def halves(self):
        return [(w, h) for w in PAIR for h in PAIR]

    def block(self, w, k, b, h):
        cols = part(h, HW)
        return self.ub.at[k, :, b, :, cols] if w else self.gb.at[k, b, :, :, cols]

    def own(self, w, k, b, j, h):
        cols = part(h, HW)
        return f32(self.ub[k, j, b, :, cols] if w else self.gb[k, b, j, :, cols])

    def c1(self, c):
        k, out = lax.rem(c, 2), []
        for w, h in self.halves():
            first, _ = partners(self.outer(w), h)
            for i, b in enumerate(passed(self.outer(w), h)):
                out.append((self.block(w, k, b, h), self.r1.at[w, k, h, i], self.at_outer(w, first)))
        return self.copies("c1", c, out)

    def c2(self, c):
        k = lax.rem(c, 2)
        return self.copies("c2", c, [(self.s2.at[w, h], self.r2.at[w, k, h], self.at_outer(w, partners(self.outer(w), h)[1])) for w, h in self.halves()])

    def c3(self, c):
        k = lax.rem(c, 2)
        return self.copies("c3", c, [(self.s3.at[w, h], self.r3.at[w, k, h], self.at_inner(w, partners(self.inner(w), h)[0])) for w, h in self.halves()])

    def c4(self, c):
        k = lax.rem(c, 2)
        return self.copies("c4", c, [(self.s4.at[w, h], self.r4.at[w, k, h], self.at_inner(w, partners(self.inner(w), h)[1])) for w, h in self.halves()])

    def cf(self, c):
        zs = [self.up_z(i) for i in range(1, 8)]
        return self.copies("cf", c, [(self.zs.at[z], self.fz.at[i], self.at(z=z)) for i, z in enumerate(zs)])

    def w1(self, c):
        go(self.c1(c))

    def w2(self, c):
        arrive(self.c1(c))
        k = lax.rem(c, 2)
        for w, h in self.halves():
            _, b = partners(self.outer(w), h)
            for j in FOUR:
                self.s2[w, h, j] = b16(self.own(w, k, b, j, h) + f32(self.r1[w, k, h, 1, j]))
        go(self.c2(c))
        leave(self.c1(c))

    def w3(self, c):
        arrive(self.c2(c))
        k = lax.rem(c, 2)
        for w, h in self.halves():
            p, q = self.outer(w), self.inner(w)

            def total(j):
                return self.own(w, k, p, j, h) + f32(self.r1[w, k, h, 0, j]) + f32(self.r2[w, k, h, j])

            for i, j in enumerate(passed(q, h)):
                self.s3[w, h, i] = b16(total(j))
            for i, j in enumerate(kept(q, h)):
                self.keep[w, h, i] = total(j)
        go(self.c3(c))
        leave(self.c2(c))

    def w4(self, c):
        arrive(self.c3(c))
        k = lax.rem(c, 2)
        for w, h in self.halves():
            self.s4[w, h] = b16(self.keep[w, h, 1] + f32(self.r3[w, k, h, 1]))
            self.keep[w, h, 0] += f32(self.r3[w, k, h, 0])
        go(self.c4(c))
        leave(self.c3(c))

    def w5(self, c):
        arrive(self.c4(c))
        k = lax.rem(c, 2)
        for w, h in self.halves():
            v = self.keep[w, h, 0] + f32(self.r4[w, k, h])
            for z in EIGHT:
                self.zf[z, w, h] = v[4 * z : 4 * z + 4]
                self.zs[z, w, h] = b16(v[4 * z : 4 * z + 4])
        self.zo[...] = self.zf[self.z]
        go(self.cf(c))
        leave(self.c4(c))

    def w6(self, c):
        arrive(self.cf(c))
        l, ci = layer_of(c), lax.rem(c, CHUNKS)
        for w, h in self.halves():
            wb, m, v, mo, vo = (getattr(self, s + "gu"[w]) for s in ("w", "m", "v", "mo", "vo"))
            g = self.zo[w, h]
            for i in range(7):
                g = g + f32(self.fz[i, w, h])
            cols = rows_of(2 * ci + h, HW)
            new, mo[l, :, cols], vo[l, :, cols] = adamw(f32(wb[l, :, cols]), m[l, :, cols], v[l, :, cols], f32(b16(g)))
            self.nb[w, h] = new
            self.wz[self.z, w, h] = new
        go(self.a0(c))
        leave(self.cf(c))


    def a0(self, c, get=False):
        zs = [self.up_z(-i if get else i) for i in range(1, 8)]
        return self.copies("a0", c, [(self.nb, self.wz.at[z if get else self.z], self.at(z=z)) for z in zs])

    def cols(self, c, h):
        return rows_of(2 * lax.rem(c, CHUNKS) + h, HW)

    def oblock(self, w, c, b, h):
        l, cols = layer_of(c), self.cols(c, h)
        return self.ou.at[l, b, self.y, :, cols] if w else self.og.at[l, self.x, b, :, cols]

    def obig(self, w, c, b, h):
        l, cols = layer_of(c), self.cols(c, h)
        return self.ou.at[l, :, b, :, cols] if w else self.og.at[l, b, :, :, cols]

    def a1(self, c, get=False):
        out = []
        for w, h in self.halves():
            _, q = partners(self.inner(w), h)
            out.append((self.slab.at[w, h], self.oblock(w, c, q if get else self.inner(w), h), self.at_inner(w, q)))
        return self.copies("a1", c, out)

    def placed(self, c):
        return [pltpu.make_async_copy(self.slab.at[w, h], self.oblock(w, c, self.inner(w), h), self.lsem.at[w, h]) for w, h in self.halves()]

    def a2(self, c, get=False):
        out = []
        for w, h in self.halves():
            first, _ = partners(self.inner(w), h)
            refs = [self.oblock(w, c, b, h) for b in (passed if get else kept)(self.inner(w), h)]
            out += [(ref, ref, self.at_inner(w, first)) for ref in refs]
        return self.copies("a2", c, out)

    def a3(self, c, get=False):
        out = []
        for w, h in self.halves():
            _, q = partners(self.outer(w), h)
            ref = self.obig(w, c, q if get else self.outer(w), h)
            out.append((ref, ref, self.at_outer(w, q)))
        return self.copies("a3", c, out)

    def a4(self, c, get=False):
        out = []
        for w, h in self.halves():
            first, _ = partners(self.outer(w), h)
            refs = [self.obig(w, c, b, h) for b in (passed if get else kept)(self.outer(w), h)]
            out += [(ref, ref, self.at_outer(w, first)) for ref in refs]
        return self.copies("a4", c, out)

    def w7(self, c):
        arrive(self.a0(c, True))
        for w, h in self.halves():
            for z in EIGHT:
                self.slabf[w, h, 4 * z : 4 * z + 4] = f32(self.wz[z, w, h])
            self.slab[w, h] = b16(self.slabf[w, h])
        go(self.a1(c) + self.placed(c))
        leave(self.a0(c))

    def w8(self, c):
        arrive(self.a1(c, True))
        for p in self.placed(c):
            p.wait()
        go(self.a2(c))
        leave(self.a1(c))

    def w9(self, c):
        self.hand_on(self.a2, self.a3, c)

    def w10(self, c):
        self.hand_on(self.a3, self.a4, c)

    def w11(self, c):
        arrive(self.a4(c, True))
        leave(self.a4(c))

    def hand_on(self, before, after, c):
        arrive(before(c, True))
        go(after(c))
        leave(before(c))


    def ring(self, c, s):
        k, out = lax.rem(c, 2), []
        for h in PAIR:
            b, to = (self.up_z(1 + s), self.up_z(-1)) if h else (self.up_z(-1 - s), self.up_z(1))
            src = self.rz.at[k, h, s - 1] if s else self.db.at[k, :, b, :, part(h, HD)]
            out.append((src, self.rz.at[k, h, s], self.at(z=to)))
        return self.ringed("ring", c, s, out)

    def ringed(self, name, c, s, moves):
        base = FIRST[name] + lax.rem(c, 2) * COUNTS[name] + 2 * s
        return [self.copy(base + i, *move) for i, move in enumerate(moves)]

    def d0(self, c):
        go(self.ring(c, 0))

    def turn_ring(self, c, s):
        arrive(self.ring(c, s - 1))
        k = lax.rem(c, 2)
        for h in PAIR:
            b = self.up_z(1 + s) if h else self.up_z(-1 - s)
            for j in FOUR:
                self.rz[k, h, s - 1, j] = b16(f32(self.rz[k, h, s - 1, j]) + f32(self.db[k, j, b, :, part(h, HD)]))
        go(self.ring(c, s))
        leave(self.ring(c, s - 1))

    def dy1(self, c):
        k = lax.rem(c, 2)
        return self.copies("dy1", c, [(self.sdy1.at[h], self.rdy1.at[k, h], self.at(y=partners(self.y, h)[0])) for h in PAIR])

    def dy2(self, c):
        k = lax.rem(c, 2)
        return self.copies("dy2", c, [(self.sdy2.at[h], self.rdy2.at[k, h], self.at(y=partners(self.y, h)[1])) for h in PAIR])

    def d7(self, c):
        arrive(self.ring(c, 6))
        k = lax.rem(c, 2)
        for h in PAIR:

            def total(j):
                return f32(self.rz[k, h, 6, j]) + f32(self.db[k, j, self.z, :, part(h, HD)])

            for i, j in enumerate(passed(self.y, h)):
                self.sdy1[h, i] = b16(total(j))
            for i, j in enumerate(kept(self.y, h)):
                self.kdy[h, i] = total(j)
        go(self.dy1(c))
        leave(self.ring(c, 6))

    def d8(self, c):
        arrive(self.dy1(c))
        k = lax.rem(c, 2)
        for h in PAIR:
            self.sdy2[h] = b16(self.kdy[h, 1] + f32(self.rdy1[k, h, 1]))
            self.kdy[h, 0] += f32(self.rdy1[k, h, 0])
        go(self.dy2(c))
        leave(self.dy1(c))

    def away(self, c):
        return self.up_x(-lax.rem(c, CHUNKS))

    def owner_sem(self, name, c):
        return FIRST[name] + lax.rem(c, 2) * COUNTS[name] - 1

    def dx(self, c):
        i = self.away(c)
        return self.copy(self.owner_sem("dx", c) + i, self.xb, self.fx.at[layer_of(c), i - 1], self.at(x=lax.rem(c, CHUNKS)))

    def dx_in(self, c, i):
        return self.copy(self.owner_sem("dx", c) + i, self.xb, self.fx.at[layer_of(c), i - 1], self.at(x=self.up_x(i)))

    def dblock(self, c, y, z):
        return self.od.at[layer_of(c), lax.rem(c, CHUNKS), y, z]

    def ex(self, c, i, to):
        return self.copy(self.owner_sem("ex", c) + i, self.nd, self.dblock(c, self.y, self.z), self.at(x=to))

    def placed_down(self, c):
        return pltpu.make_async_copy(self.nd, self.dblock(c, self.y, self.z), self.lsem.at[2, 0])

    def d9(self, c):
        arrive(self.dy2(c))
        k = lax.rem(c, 2)
        for h in PAIR:
            self.xo[:, part(h, HD)] = self.kdy[h, 0] + f32(self.rdy2[k, h])
        self.xb[...] = b16(self.xo[...])

        @pl.when(self.away(c) > 0)
        def _():
            self.dx(c).start()

        leave(self.dy2(c))

    def d10(self, c):
        l = layer_of(c)

        @pl.when(self.away(c) > 0)
        def _():
            self.dx(c).wait_send()

        @pl.when(self.away(c) == 0)
        def _():
            for i in range(1, 4):
                self.dx_in(c, i).wait_recv()
            g = self.xo[...]
            for i in range(3):
                g = g + f32(self.fx[l, i])
            self.nd[...], self.mod[l], self.vod[l] = adamw(f32(self.wd[l]), self.md[l], self.vd[l], f32(b16(g)))
            self.placed_down(c).start()
            for i in range(1, 4):
                self.ex(c, i, self.up_x(i)).start()

    def d11(self, c):
        @pl.when(self.away(c) > 0)
        def _():
            self.ex(c, self.away(c), lax.rem(c, CHUNKS)).wait_recv()

        @pl.when(self.away(c) == 0)
        def _():
            self.placed_down(c).wait()
            for i in range(1, 4):
                self.ex(c, i, self.up_x(i)).wait_send()

        go(self.ey1(c))

    def ey1(self, c, get=False):
        out = []
        for h in PAIR:
            _, q = partners(self.y, h)
            ref = self.dblock(c, q if get else self.y, self.z).at[:, part(h, HD)]
            out.append((ref, ref, self.at(y=q)))
        return self.copies("ey1", c, out)

    def ey2(self, c, get=False):
        out = []
        for h in PAIR:
            first, _ = partners(self.y, h)
            refs = [self.dblock(c, b, self.z).at[:, part(h, HD)] for b in (passed if get else kept)(self.y, h)]
            out += [(ref, ref, self.at(y=first)) for ref in refs]
        return self.copies("ey2", c, out)

    def back(self, c, s, get=False):
        out = []
        for h in PAIR:
            b, to = (self.up_z(s + get), self.up_z(-1)) if h else (self.up_z(-s - get), self.up_z(1))
            ref = self.od.at[layer_of(c), lax.rem(c, CHUNKS), :, b, :, part(h, HD)]
            out.append((ref, ref, self.at(z=to)))
        return self.ringed("back", c, s, out)

    def d12(self, c):
        self.hand_on(self.ey1, self.ey2, c)

    def d13(self, c):
        arrive(self.ey2(c, True))
        go(self.back(c, 0))
        leave(self.ey2(c))

    def ring_back(self, c, s):
        arrive(self.back(c, s - 1, True))
        go(self.back(c, s))
        leave(self.back(c, s - 1))

    def d20(self, c):
        arrive(self.back(c, 6, True))
        leave(self.back(c, 6))


    def weights(self, i):
        l = jnp.where((i >= CHUNKS) & (i < LAST), 1, 0)
        k, ci = lax.rem(i, 2), lax.rem(i, CHUNKS)
        hidden = rows_of(ci, CW)
        pairs = ((self.w_gate.at[l, :, hidden], self.wcg), (self.w_up.at[l, :, hidden], self.wcu), (self.w_down.at[l, hidden], self.wcd))
        return [pltpu.make_async_copy(src, dst.at[k], self.wsem.at[k, i]) for i, (src, dst) in enumerate(pairs)]

    def scale(self, h):
        return lax.rsqrt(jnp.mean(h * h, -1, keepdims=True) + 1e-6)

    def sweep(self, body, n=SUB, lo=0, hi=None):
        def step(t, carry):
            body(rows_of(t, n))
            return carry

        lax.fori_loop(lo, TOK // n if hi is None else hi, step, 0)

    def turn(self, src, dst):
        for i in EIGHT:
            for j in PAIR:
                dst[part(j, SUB), part(i, SUB)] = b16(dot_t(self.eye[...], src[part(i, SUB), part(j, SUB)]))

    def normed(self, rows, h):
        h = f32(h)
        self.a[rows] = b16(h * self.scale(h))

    def start(self):
        i, j = (lax.broadcasted_iota(jnp.int32, (SUB, SUB), axis) for axis in PAIR)
        self.eye[...] = b16(jnp.where(i == j, 1.0, 0.0))
        self.sweep(lambda rows: self.normed(rows, self.xv[rows]))

    def forward(self, i):
        k = lax.rem(i, 2)

        def body(rows):
            a = self.a[rows]
            for n in range(CW // SUB):
                cols = part(n, SUB)
                g = dot(a, self.wcg[k, :, cols])
                u = dot(a, self.wcu[k, :, cols])
                s = 0.5 * jnp.tanh(0.5 * g) + 0.5
                self.act[rows, cols] = b16(g * s * u)
            y = dot(self.act[rows], self.wcd[k])

            @pl.when(i == 0)
            def _():
                self.acc[rows] = y

            @pl.when(i > 0)
            def _():
                self.acc[rows] += y

        self.sweep(body, T)

    def layer_up(self):
        def body(rows):
            h = b16(f32(self.xv[rows]) + f32(b16(self.acc[rows])))
            self.h[rows] = h
            self.normed(rows, h)

        self.sweep(body)
        self.turn(self.a, self.at_)
        self.turn(self.dh, self.dht)

    def layer_down(self):
        def body(rows):
            h = f32(self.h[rows])
            s = self.scale(h)
            ct = f32(b16(self.acc[rows]))
            d = ct * s - h * (s * s * s * jnp.mean(ct * h, -1, keepdims=True))
            self.dh[rows] = b16(f32(self.dh[rows]) + f32(b16(d)))
            self.normed(rows, self.xv[rows])

        self.sweep(body)
        self.turn(self.a, self.at_)
        self.turn(self.dh, self.dht)

    def tiles(self, k, c, lo, hi):
        def body(rows):
            a, dh = self.a[rows], self.dh[rows]
            for n in range(CW // SUB):
                cols = part(n, SUB)
                g = dot(a, self.wcg[k, :, cols])
                u = dot(a, self.wcu[k, :, cols])
                d = f32(b16(dot_t(dh, self.wcd[k, cols])))
                s = 0.5 * jnp.tanh(0.5 * g) + 0.5
                sg = g * s
                self.act[rows, cols] = b16(sg * u)
                self.du[rows, cols] = b16(d * sg)
                self.dg[rows, cols] = b16(d * u * (s + sg * (1.0 - s)))

            @pl.when(c < CHUNKS)
            def _():
                v = dot_t(self.dg[rows], self.wcg[k]) + dot_t(self.du[rows], self.wcu[k])

                @pl.when(c == 0)
                def _():
                    self.acc[rows] = v

                @pl.when(c > 0)
                def _():
                    self.acc[rows] += v

        self.sweep(body, T, lo, hi)

    def grads_down(self, k):
        for n in range(CW // SUB):
            v = dot_t(self.eye[...], b16(dot(self.dht[...], self.act[:, part(n, SUB)])))
            for i in range(SUB // 8):
                q, o = divmod(n * SUB + i * 8, 24)
                self.db[k, q // 8, q % 8, o : o + 8, :] = b16(v[i * 8 : i * 8 + 8])

    def grads(self, k, n):
        cols = part(n, SUB)
        for src, dst in ((self.dg, self.gb), (self.du, self.ub)):
            dst[k, :, :, :, cols] = b16(dot(self.at_[...], src[:, cols])).reshape(*GU, SUB)


def vm(*shape, dtype=BF16):
    return pltpu.VMEM(shape, dtype)


GU = (4, 4, 32)
DN = (4, 8, 24, D)
SCRATCH = dict(
    xv=vm(TOK, D), h=vm(TOK, D), a=vm(TOK, D), at_=vm(D, TOK), dh=vm(TOK, D), dht=vm(D, TOK), acc=vm(TOK, D, dtype=F32),
    act=vm(TOK, CW), dg=vm(TOK, CW), du=vm(TOK, CW), eye=vm(SUB, SUB), wcg=vm(2, D, CW), wcu=vm(2, D, CW), wcd=vm(2, CW, D),
    gb=vm(2, *GU, CW), ub=vm(2, *GU, CW), db=vm(2, *DN),
    r1=vm(2, 2, 2, 2, 4, 32, HW), s2=vm(2, 2, 4, 32, HW), r2=vm(2, 2, 2, 4, 32, HW),
    s3=vm(2, 2, 2, 32, HW), r3=vm(2, 2, 2, 2, 32, HW), keep=vm(2, 2, 2, 32, HW, dtype=F32), s4=vm(2, 2, 32, HW), r4=vm(2, 2, 2, 32, HW),
    zf=vm(8, 2, 2, 4, HW, dtype=F32), zs=vm(8, 2, 2, 4, HW), zo=vm(2, 2, 4, HW, dtype=F32), fz=vm(7, 2, 2, 4, HW),
    nb=vm(2, 2, 4, HW), wz=vm(8, 2, 2, 4, HW), slabf=vm(2, 2, 32, HW, dtype=F32), slab=vm(2, 2, 32, HW),
    rz=vm(2, 2, 7, 4, 24, HD), sdy1=vm(2, 2, 24, HD), rdy1=vm(2, 2, 2, 24, HD), kdy=vm(2, 2, 24, HD, dtype=F32), sdy2=vm(2, 24, HD),
    rdy2=vm(2, 2, 24, HD), xb=vm(24, D), xo=vm(24, D, dtype=F32), fx=vm(2, 3, 24, D), nd=vm(24, D),
    ssem=pltpu.SemaphoreType.DMA((SEMS,)), rsem=pltpu.SemaphoreType.DMA((SEMS,)), lsem=pltpu.SemaphoreType.DMA((3, 2)),
    wsem=pltpu.SemaphoreType.DMA((2, 3)), xsem=pltpu.SemaphoreType.DMA((2,)),
)
HBM_IN = ("x_in", "dy", "w_gate", "w_up", "w_down")
VMEM_IN = ("wg", "wu", "wd", "mg", "mu", "md", "vg", "vu", "vd")
OUT = ("og", "ou", "od", "mog", "mou", "mod", "vog", "vou", "vod")

SLOTS = 8
RINGS = range(1, 7)
EVENTS = {"d0": 4, "w1": 7, "w2": 10, "w3": 12, "w4": 14, "w5": 16, "d7": 18, "w6": 18, "d8": 20, "w7": 20, "d9": 22, "w8": 22}
EVENTS |= {"d10": 24, "w9": 24, "d11": 26, "w10": 27, "d12": 28, "d13": 30, "w11": 30, "d20": 44}
EVENTS |= {("turn_ring", s): 4 + 2 * s for s in RINGS} | {("ring_back", s): 30 + 2 * s for s in RINGS}
SPAN = max(EVENTS.values()) // SLOTS


def kernel(*refs):
    names = HBM_IN + VMEM_IN + OUT + tuple(SCRATCH)
    q = Step(dict(zip(names, refs, strict=True)))
    first = [pltpu.make_async_copy(src.at[0], dst, q.xsem.at[i]) for i, (src, dst) in enumerate(((q.x_in, q.xv), (q.dy, q.dh)))]
    go(first + q.weights(0))
    q.barrier()
    first[0].wait()
    q.start()

    def forward(i, carry):
        go(q.weights(i + 1))
        for w in q.weights(i):
            w.wait()
        q.forward(i)
        return carry

    lax.fori_loop(0, CHUNKS, forward, 0)
    first[1].wait()
    q.layer_up()

    def chunk(c, carry):
        k = lax.rem(c, 2)

        @pl.when(c < LAST - 1)
        def _():
            go(q.weights(c + CHUNKS + 1))

        @pl.when(c < LAST)
        def _():
            for w in q.weights(c + CHUNKS):
                w.wait()

        @pl.when(c == CHUNKS)
        def _():
            q.layer_down()

        pieces = [lambda t=t: q.tiles(k, c, t, t + 1) for t in FOUR] + [lambda: q.grads_down(k)] + [lambda n=n: q.grads(k, n) for n in range(CW // SUB)]
        for slot, piece in enumerate(pieces):

            @pl.when(c < LAST)
            def _():
                run("compute", piece)

            for event, place in sorted(EVENTS.items(), key=lambda item: -item[1]):
                if place % SLOTS == slot:
                    back = place // SLOTS

                    @pl.when((c >= back) & (c < LAST + back))
                    def _():
                        name, args = (event, ()) if isinstance(event, str) else (event[0], event[1:])
                        run(name, getattr(q, name), c - back, *args)

        return carry

    lax.fori_loop(0, LAST + SPAN, chunk, 0)


def run(name, f, *args):
    f(*args)


def solution(mesh):
    def local(x, dy, wg, wu, wd, *mv):
        d = lax.axis_index("dp")
        blocks = [lax.dynamic_slice_in_dim(w, d * n, n, 1) for w, n in ((wg, 4), (wu, 4), (wd, 24))]
        hbm, vmem = (pl.BlockSpec(memory_space=s) for s in (pl.ANY, pltpu.VMEM))
        news = [jax.ShapeDtypeStruct((2, *s), BF16) for s in ((*GU, FF), (*GU, FF), (4, *DN))]
        moments = [jax.ShapeDtypeStruct(t.shape, F32) for t in mv]
        out = pl.pallas_call(
            kernel,
            name="step",
            out_shape=news + moments,
            in_specs=[hbm] * 5 + [vmem] * 9,
            out_specs=[hbm] * 3 + [vmem] * 6,
            scratch_shapes=list(SCRATCH.values()),
            compiler_params=pltpu.CompilerParams(collective_id=1, has_side_effects=True, vmem_limit_bytes=67043328),
        )(x, dy, wg, wu, wd, *blocks, *mv)
        return *(t.reshape(w.shape) for t, w in zip(out, (wg, wu, wd))), *out[3:]

    rows, whole = P(None, "dp", None), P()
    return jax.shard_map(
        local,
        mesh=mesh,
        in_specs=(P(("rep", "dp"), None, None),) * 2 + (whole,) * 3 + (rows,) * 6,
        out_specs=(P("rep", None, None),) * 3 + (P("rep", "dp", None),) * 6,
        check_vma=False,
    )
```

time: 2250 us -> 317 us (0.14)
  waiting for transfers between devices: 1130 us -> 0 us
  blocking collectives: 776 us -> 0 us
  Pallas kernels: 0 us -> 296 us
  matrix products: 226 us -> 0 us
  other arithmetic: 55.7 us -> 0.01 us
    unnamed x7 -> x0, waiting for transfers between devices: 787 us -> none
    unnamed x1 -> x0, blocking collectives: 776 us -> none
    reshape x3 -> x0, waiting for transfers between devices: 345 us -> none  [step(): t.reshape(-1, *t.shape[2:])]
    pallas_call x0 -> x1, Pallas kernels: none -> 296 us  [local(): pl.pallas_call(kernel, name='step', out_shape=news + moments, in_specs=[h...]
    dot_general x15 -> x0, matrix products: 226 us -> none  [the longest x5 84.7 us: layer(): up = jnp.dot(a, w['w_up'], preferred_element_type=jnp.float32)]
    unnamed x4 -> x1, other arithmetic: 46.9 us -> 0.01 us
  transfers between devices with their start and end apart: 5 -> 0, of which waited for: 4 -> 0; matrix products, arithmetic and copies ran while one was open for 6% -> 0% of each run, Pallas kernels for 0% -> 0%
where the time goes in v1:
time: 317 us
  Pallas kernels  296 us (93%)
  local copies, waits for them, and re-layouts  20.7 us (7%)
    pallas_call x1, Pallas kernels, local(): pl.pallas_call(kernel, name='step', out_shape=news + moments, in_specs=[h...  296 us
    unnamed x27, local copies, waits for them, and re-layouts  17.7 us

profile of v1, /device:TPU:2, one launch (start us, length us, event | category | flops | bytes accessed | tf_op | source)
XLA Modules:
  0.0 317.2 jit_solution(5129270163581161925)
XLA Ops:
  0.6 1.4 constant_dynamic-slice_fusion.refs_7_
  2.1 1.6 constant_dynamic-slice_fusion.1
  3.7 295.7 %step.1 = (bf16[2,4,4,32,3072]{4,3,2,1,0:T(8,128)(2,1)}, bf16[2,4,4,32,3072]{4,3,2,1,0:T(8,128)(2,1)}, bf16[2,4,4,8,24,512]{5,4,3,2,1,0:T(8,128)(2,1)}, f32[2,4,...) custom-call(bf16[1,2048,512]{2,1,0:T(8,128)(2,1)} %refs_0_.1, ...), custom_call_target="tpu_custom_call" | custom-call | tf_op jit(solution)/shard_map/step/pallas_call | solution.py:719
  299.4 0.0 copy-start
  299.4 0.0 slice-start
  299.4 6.6 %copy.29 = bf16[2,512,3072]{2,1,0:T(8,128)(2,1)} copy(bf16[2,512,3072]{2,1,0:T(8,128)(2,1)} %bitcast.7) | data formatting | bytes 12582912
  306.0 0.0 copy-done
  306.0 0.0 slice-start.1
  306.0 3.2 %copy.30 = bf16[2,512,3072]{2,1,0:T(8,128)(2,1)} copy(bf16[2,512,3072]{2,1,0:T(8,128)(2,1)S(1)} %bitcast.6) | data formatting | bytes 12582912
  309.2 0.0 slice-done
  309.2 1.3 slice-done.1
  310.6 0.0 copy-start.6
  310.6 0.0 copy-start.5
  310.6 0.0 copy-start.4
  310.6 0.0 copy-start.3
  310.6 0.0 copy-start.2
  310.6 0.0 copy-start.1
  310.6 2.7 copy.31
  313.3 0.0 copy-done.6
  313.3 0.6 copy.32
  313.9 0.0 copy-done.5
  313.9 0.6 copy.33
  314.6 0.0 copy-done.4
  314.6 0.6 copy.34
  315.2 0.0 copy-done.3
  315.2 0.6 copy.35
  315.9 0.0 copy-done.2
  315.9 0.6 copy.36
  316.5 0.0 copy-done.1
  316.5 0.6 copy.37
  (1 shorter events, 0.0 us)
Async XLA Ops:
  299.4 6.6 %copy-start = (bf16[2,4,4,32,3072]{4,3,2,1,0:T(8,128)(2,1)S(1)}, bf16[2,4,4,32,3072]{4,3,2,1,0:T(8,128)(2,1)}, u32[]{:S(2)}) copy-start(bf16[2,4,4,32,3072]{4,3,2,1,0:T(8,128)(2,1)} %get-tuple-element.19) | copy-start | bytes 18874372
  299.4 9.8 %slice-start = ((s8[6291456]{0:T(1024)(128)(4,1)}), s8[4194304]{0:T(1024)(128)(4,1)S(1)}, s32[]{:S(2)}) async-start(s8[6291456]{0:T(1024)(128)(4,1)} %bitcast.3), calls=%async_computation | async-start | bytes 8388608
  306.0 4.5 %slice-start.1 = ((s8[6291456]{0:T(1024)(128)(4,1)}), s8[2097152]{0:T(1024)(128)(4,1)S(1)}, s32[]{:S(2)}) async-start(s8[6291456]{0:T(1024)(128)(4,1)} %bitcast.3), calls=%async_computation.1 | async-start | bytes 4194304
  310.6 2.7 copy-start.6
  310.6 3.4 %copy-start.5 = (f32[2,4,3072]{2,1,0:T(4,128)S(1)}, f32[2,4,3072]{2,1,0:T(4,128)}, u32[]{:S(2)}) copy-start(f32[2,4,3072]{2,1,0:T(4,128)} %get-tuple-element.42) | copy-start | bytes 294916
  310.6 4.0 %copy-start.4 = (f32[2,24,512]{2,1,0:T(8,128)S(1)}, f32[2,24,512]{2,1,0:T(8,128)}, u32[]{:S(2)}) copy-start(f32[2,24,512]{2,1,0:T(8,128)} %get-tuple-element.43) | copy-start | bytes 294916
  310.6 4.7 %copy-start.3 = (f32[2,4,3072]{2,1,0:T(4,128)S(1)}, f32[2,4,3072]{2,1,0:T(4,128)}, u32[]{:S(2)}) copy-start(f32[2,4,3072]{2,1,0:T(4,128)} %get-tuple-element.44) | copy-start | bytes 294916
  310.6 5.3 %copy-start.2 = (f32[2,4,3072]{2,1,0:T(4,128)S(1)}, f32[2,4,3072]{2,1,0:T(4,128)}, u32[]{:S(2)}) copy-start(f32[2,4,3072]{2,1,0:T(4,128)} %get-tuple-element.45) | copy-start | bytes 294916
  310.6 5.9 %copy-start.1 = (f32[2,24,512]{2,1,0:T(8,128)S(1)}, f32[2,24,512]{2,1,0:T(8,128)}, u32[]{:S(2)}) copy-start(f32[2,24,512]{2,1,0:T(8,128)} %get-tuple-element.46) | copy-start | bytes 294916

commit v2 on v1

v2 whole, which is shorter than its diff:
```python
import jax
import jax.numpy as jnp
from jax import lax
from jax.experimental import pallas as pl
from jax.experimental.pallas import tpu as pltpu
from jax.sharding import PartitionSpec as P

MESH = pl.DeviceIdType.MESH
F32, BF16 = jnp.float32, jnp.bfloat16
TOK, D, FF = 2048, 512, 3072
CW = 768
HW = CW // 2
HF = FF // 2
HD = D // 2
LN = 128
CHUNKS = FF // CW
LAST = 2 * CHUNKS
PAIR = (0, 1)
FOUR = range(4)
EIGHT = range(8)
T = 512
SUB = 256


def f32(v):
    return v.astype(F32)


def b16(v):
    return v.astype(BF16)


def dot(a, b):
    return jnp.dot(a, b, preferred_element_type=F32)


def dot_t(a, b):
    return lax.dot_general(a, b, (((1,), (1,)), ((), ())), preferred_element_type=F32)


def rows_of(t, n):
    return pl.ds(pl.multiple_of(t * n, n), n)


def part(i, n):
    return pl.ds(i * n, n)


def flip(p):
    return p + 1 - 2 * lax.rem(p, 2)


def mirror(p):
    return 3 - p


def partners(p, half):
    return (mirror(p), flip(p)) if half else (flip(p), mirror(p))


def passed(p, half):
    first, _ = partners(p, half)
    return first, partners(first, half)[1]


def kept(p, half):
    return p, partners(p, half)[1]


def layer_of(c):
    return jnp.where(c < CHUNKS, 1, 0)


def go(copies):
    for c in copies:
        c.start()


def arrive(copies):
    for c in copies:
        c.wait_recv()


def leave(copies):
    for c in copies:
        c.wait_send()


def adamw(w, m, v, g):
    m = 0.9 * m + 0.1 * g
    v = 0.95 * v + 0.05 * g * g
    step = m * lax.rsqrt(v + 1e-8) + 0.1 * w
    return b16(w - 0.02 * step), m, v


COUNTS = dict(c1=8, c2=4, c3=6, cf=7, a0=7, a1=6, a3=4, a4=8, r0=2, r1=4, r2=2, r3=2, dy=3, dx=3, ex=3, ey=3, b0=2, b1=2, b2=2, b3=2)
FIRST = {}
SEMS = 0
for _name, _n in COUNTS.items():
    FIRST[_name] = SEMS
    SEMS += 2 * _n
OTHERS = (1, 2, 3)


class Step:
    def __init__(self, refs):
        self.__dict__.update(refs)
        d = lax.axis_index("dp")
        self.rep = lax.axis_index("rep")
        self.x, self.y, self.z = d // 32, lax.rem(d // 8, 4), lax.rem(d, 8)


    def at(self, x=None, y=None, z=None):
        x = self.x if x is None else x
        y = self.y if y is None else y
        z = self.z if z is None else z
        return (self.rep, x * 32 + y * 8 + z)

    def up_z(self, i):
        return lax.rem(self.z + i + 16, 8)

    def up_x(self, i):
        return lax.rem(self.x + i + 4, 4)

    def up_y(self, i):
        return lax.rem(self.y + i + 4, 4)

    def up_inner(self, w, i):
        return self.up_x(i) if w else self.up_y(i)

    def copy(self, sem, src, dst, dev):
        return pltpu.make_async_remote_copy(
            src_ref=src, dst_ref=dst, send_sem=self.ssem.at[sem], recv_sem=self.rsem.at[sem], device_id=dev, device_id_type=MESH
        )

    def copies(self, name, c, moves):
        base = FIRST[name] + lax.rem(c, 2) * COUNTS[name]
        return [self.copy(base + i, *move) for i, move in enumerate(moves)]

    def peers(self):
        out = [self.at(z=self.up_z(i)) for i in range(1, 8)]
        return out + [self.at(x=self.up_x(i)) for i in OTHERS] + [self.at(y=self.up_y(i)) for i in OTHERS]

    def greet(self):
        b = pltpu.get_barrier_semaphore()
        for q in self.peers():
            pl.semaphore_signal(b, inc=1, device_id=q, device_id_type=MESH)

    def greeted(self):
        pl.semaphore_wait(pltpu.get_barrier_semaphore(), len(self.peers()))


    def outer(self, w):
        return self.y if w else self.x

    def inner(self, w):
        return self.x if w else self.y

    def at_outer(self, w, p):
        return self.at(y=p) if w else self.at(x=p)

    def at_inner(self, w, p):
        return self.at(x=p) if w else self.at(y=p)

    def halves(self):
        return [(w, h) for w in PAIR for h in PAIR]

    def block(self, w, k, b, h):
        cols = part(h, HW)
        return self.ub.at[k, :, b, :, cols] if w else self.gb.at[k, b, :, :, cols]

    def own(self, w, k, b, j, h):
        cols = part(h, HW)
        return f32(self.ub[k, j, b, :, cols] if w else self.gb[k, b, j, :, cols])

    def c1(self, c):
        k, out = lax.rem(c, 2), []
        for w, h in self.halves():
            first, _ = partners(self.outer(w), h)
            for i, b in enumerate(passed(self.outer(w), h)):
                out.append((self.block(w, k, b, h), self.r1.at[w, k, h, i], self.at_outer(w, first)))
        return self.copies("c1", c, out)

    def c2(self, c):
        k = lax.rem(c, 2)
        return self.copies("c2", c, [(self.s2.at[w, h], self.r2.at[w, k, h], self.at_outer(w, partners(self.outer(w), h)[1])) for w, h in self.halves()])

    def c3(self, c):
        k, out = lax.rem(c, 2), []
        for w in PAIR:
            for i in OTHERS:
                j = self.up_inner(w, i)
                out.append((self.s3.at[w, j], self.r3.at[w, k, i - 1], self.at_inner(w, j)))
        return self.copies("c3", c, out)

    def cf(self, c):
        zs = [self.up_z(i) for i in range(1, 8)]
        return self.copies("cf", c, [(self.zs.at[z], self.fz.at[i], self.at(z=z)) for i, z in enumerate(zs)])

    def w1(self, c):
        go(self.c1(c))

    def w2(self, c):
        arrive(self.c1(c))
        k = lax.rem(c, 2)
        for w, h in self.halves():
            _, b = partners(self.outer(w), h)
            for j in FOUR:
                self.s2[w, h, j] = b16(self.own(w, k, b, j, h) + f32(self.r1[w, k, h, 1, j]))
        go(self.c2(c))
        leave(self.c1(c))

    def wi(self, c):
        arrive(self.c2(c))
        k = lax.rem(c, 2)
        for w, h in self.halves():

            def total(j):
                return self.own(w, k, self.outer(w), j, h) + f32(self.r1[w, k, h, 0, j]) + f32(self.r2[w, k, h, j])

            for i in OTHERS:
                j = self.up_inner(w, i)
                self.s3[w, j, h] = b16(total(j))
            self.keep[w, h] = total(self.inner(w))
        go(self.c3(c))
        leave(self.c2(c))

    def wf(self, c):
        arrive(self.c3(c))
        k = lax.rem(c, 2)
        for w, h in self.halves():
            v = self.keep[w, h]
            for i in range(3):
                v = v + f32(self.r3[w, k, i, h])
            for z in EIGHT:
                self.zf[z, w, h] = v[4 * z : 4 * z + 4]
                self.zs[z, w, h] = b16(v[4 * z : 4 * z + 4])
        self.zo[...] = self.zf[self.z]
        go(self.cf(c))
        leave(self.c3(c))

    def renew(self, c):
        arrive(self.cf(c))
        l, ci = layer_of(c), lax.rem(c, CHUNKS)
        for w, h in self.halves():
            wb, m, v, mo, vo = (getattr(self, s + "gu"[w]) for s in ("w", "m", "v", "mo", "vo"))
            g = self.zo[w, h]
            for i in range(7):
                g = g + f32(self.fz[i, w, h])
            cols = rows_of(2 * ci + h, HW)
            new, mo[l, :, cols], vo[l, :, cols] = adamw(f32(wb[l, :, cols]), m[l, :, cols], v[l, :, cols], f32(b16(g)))
            self.nb[w, h] = new
            self.wz[self.z, w, h] = new
        go(self.a0(c))
        leave(self.cf(c))


    def a0(self, c, get=False):
        zs = [self.up_z(-i if get else i) for i in range(1, 8)]
        return self.copies("a0", c, [(self.nb, self.wz.at[z if get else self.z], self.at(z=z)) for z in zs])

    def cols(self, c, h):
        return rows_of(2 * lax.rem(c, CHUNKS) + h, HW)

    def obig(self, w, c, b, h):
        l, cols = layer_of(c), self.cols(c, h)
        return self.ou.at[l, :, b, :, cols] if w else self.og.at[l, b, :, :, cols]

    def orows(self, w, c, b):
        l, cols = layer_of(c), rows_of(lax.rem(c, CHUNKS), CW)
        return self.ou.at[l, b, self.y, :, cols] if w else self.og.at[l, self.x, b, :, cols]

    def a1(self, c, get=False):
        out = []
        for w in PAIR:
            for i in OTHERS:
                j = self.up_inner(w, -i if get else i)
                out.append((self.slab.at[w], self.orows(w, c, j if get else self.inner(w)), self.at_inner(w, j)))
        return self.copies("a1", c, out)

    def placed(self, c):
        return [pltpu.make_async_copy(self.slab.at[w], self.orows(w, c, self.inner(w)), self.lsem.at[w]) for w in PAIR]

    def a3(self, c, get=False):
        out = []
        for w, h in self.halves():
            _, q = partners(self.outer(w), h)
            ref = self.obig(w, c, q if get else self.outer(w), h)
            out.append((ref, ref, self.at_outer(w, q)))
        return self.copies("a3", c, out)

    def a4(self, c, get=False):
        out = []
        for w, h in self.halves():
            first, _ = partners(self.outer(w), h)
            refs = [self.obig(w, c, b, h) for b in (passed if get else kept)(self.outer(w), h)]
            out += [(ref, ref, self.at_outer(w, first)) for ref in refs]
        return self.copies("a4", c, out)

    def gi(self, c):
        arrive(self.a0(c, True))
        for w, h in self.halves():
            for z in EIGHT:
                self.slabf[w, 4 * z : 4 * z + 4, part(h, HW)] = f32(self.wz[z, w, h])
        self.slab[...] = b16(self.slabf[...])
        go(self.a1(c) + self.placed(c))
        leave(self.a0(c))

    def g1(self, c):
        arrive(self.a1(c, True))
        for p in self.placed(c):
            p.wait()
        go(self.a3(c))
        leave(self.a1(c))

    def g2(self, c):
        self.hand_on(self.a3, self.a4, c)

    def gend(self, c):
        arrive(self.a4(c, True))
        leave(self.a4(c))

    def hand_on(self, before, after, c):
        arrive(before(c, True))
        go(after(c))
        leave(before(c))


    def sides(self):
        return enumerate((self.up_z(1), self.up_z(-1)))

    def far(self, side, n):
        return self.up_z(-n if side else n)

    def dgrad(self, c, b, *cols):
        return self.db.at[(lax.rem(c, 3), slice(None), b, slice(None), *cols)]

    def cr0(self, c):
        k = lax.rem(c, 2)
        return self.copies("r0", c, [(self.dgrad(c, self.far(0, 4), part(h, HD)), self.rz0.at[k, h], self.at(z=to)) for h, to in self.sides()])

    def cr1(self, c):
        k, out = lax.rem(c, 2), []
        for h, to in self.sides():
            out.append((self.rz0.at[k, h], self.rz.at[k, 0, h, :, :, part(h, HD)], self.at(z=to)))
            out.append((self.dgrad(c, self.far(h, 3), part(1 - h, HD)), self.rz.at[k, 0, h, :, :, part(1 - h, HD)], self.at(z=to)))
        return self.copies("r1", c, out)

    def cr2(self, c):
        return self.ringed("r2", c, 1)

    def cr3(self, c):
        return self.ringed("r3", c, 2)

    def ringed(self, name, c, s):
        k = lax.rem(c, 2)
        return self.copies(name, c, [(self.rz.at[k, s - 1, h], self.rz.at[k, s, h], self.at(z=to)) for h, to in self.sides()])

    def d0(self, c):
        go(self.cr0(c))

    def d1(self, c):
        arrive(self.cr0(c))
        k = lax.rem(c, 2)
        for h in PAIR:
            own = self.dgrad(c, self.far(h, 3), part(h, HD))
            for j in FOUR:
                self.rz0[k, h, j] = b16(f32(self.rz0[k, h, j]) + f32(own[j]))
        go(self.cr1(c))
        leave(self.cr0(c))

    def d2(self, c):
        self.pass_on(c, self.cr1, self.cr2, 0)

    def d3(self, c):
        self.pass_on(c, self.cr2, self.cr3, 1)

    def pass_on(self, c, before, after, s):
        arrive(before(c))
        k = lax.rem(c, 2)
        for h in PAIR:
            own = self.dgrad(c, self.far(h, 2 - s))
            for j in FOUR:
                self.rz[k, s, h, j] = b16(f32(self.rz[k, s, h, j]) + f32(own[j]))
        go(after(c))
        leave(before(c))

    def cy(self, c):
        k = lax.rem(c, 2)
        ys = [self.up_y(i) for i in OTHERS]
        return self.copies("dy", c, [(self.sdy.at[y], self.rdy.at[k, i], self.at(y=y)) for i, y in enumerate(ys)])

    def dy_sum(self, c):
        arrive(self.cr3(c))
        k = lax.rem(c, 2)

        def total(j):
            return f32(self.rz[k, 2, 0, j]) + f32(self.rz[k, 2, 1, j]) + f32(self.dgrad(c, self.z)[j])

        for i in OTHERS:
            y = self.up_y(i)
            self.sdy[y] = b16(total(y))
        self.kdy[...] = total(self.y)
        go(self.cy(c))
        leave(self.cr3(c))

    def away(self, c):
        return self.up_x(-lax.rem(c, CHUNKS))

    def owner_sem(self, name, c):
        return FIRST[name] + lax.rem(c, 2) * COUNTS[name] - 1

    def to_owner(self, c, i, x):
        return self.copy(self.owner_sem("dx", c) + i, self.xb, self.fx.at[layer_of(c), i - 1], self.at(x=x))

    def dblock(self, c, y):
        return self.od.at[layer_of(c), lax.rem(c, CHUNKS), y, self.z]

    def from_owner(self, c, i, x):
        return self.copy(self.owner_sem("ex", c) + i, self.nd, self.dblock(c, self.y), self.at(x=x))

    def placed_down(self, c):
        return pltpu.make_async_copy(self.nd, self.dblock(c, self.y), self.lsem.at[2])

    def dx(self, c):
        arrive(self.cy(c))
        k = lax.rem(c, 2)
        v = self.kdy[...]
        for i in range(3):
            v = v + f32(self.rdy[k, i])
        self.xo[...] = v
        self.xb[...] = b16(v)

        @pl.when(self.away(c) > 0)
        def _():
            self.to_owner(c, self.away(c), lax.rem(c, CHUNKS)).start()

        leave(self.cy(c))

    def ex(self, c):
        l = layer_of(c)

        @pl.when(self.away(c) > 0)
        def _():
            self.to_owner(c, self.away(c), lax.rem(c, CHUNKS)).wait_send()

        @pl.when(self.away(c) == 0)
        def _():
            g = self.xo[...]
            for i in OTHERS:
                self.to_owner(c, i, self.up_x(i)).wait_recv()
                g = g + f32(self.fx[l, i - 1])
            self.nd[...], self.mod[l], self.vod[l] = adamw(f32(self.wd[l]), self.md[l], self.vd[l], f32(b16(g)))
            self.placed_down(c).start()
            for i in OTHERS:
                self.from_owner(c, i, self.up_x(i)).start()

    def ey(self, c):
        @pl.when(self.away(c) > 0)
        def _():
            self.from_owner(c, self.away(c), lax.rem(c, CHUNKS)).wait_recv()

        @pl.when(self.away(c) == 0)
        def _():
            self.placed_down(c).wait()
            for i in OTHERS:
                self.from_owner(c, i, self.up_x(i)).wait_send()

        go(self.cz(c))

    def cz(self, c, get=False):
        out = []
        for i in OTHERS:
            y = self.up_y(-i if get else i)
            ref = self.dblock(c, y if get else self.y)
            out.append((ref, ref, self.at(y=y)))
        return self.copies("ey", c, out)

    def back(self, name, n, half=False):
        def moves(c, get=False):
            out = []
            for h, to in self.sides():
                ref = self.od.at[layer_of(c), lax.rem(c, CHUNKS), :, self.far(1 - h, n + get)]
                ref = ref.at[:, :, part(h, HD)] if half else ref
                out.append((ref, ref, self.at(z=to)))
            return self.copies(name, c, out)

        return moves

    def b0(self, c):
        arrive(self.cz(c, True))
        go(self.back("b0", 0)(c))
        leave(self.cz(c))

    def b1(self, c):
        self.hand_on(self.back("b0", 0), self.back("b1", 1), c)

    def b2(self, c):
        self.hand_on(self.back("b1", 1), self.back("b2", 2), c)

    def b3(self, c):
        self.hand_on(self.back("b2", 2), self.back("b3", 3, True), c)

    def dend(self, c):
        arrive(self.back("b3", 3, True)(c, True))
        leave(self.back("b3", 3, True)(c))


    def weights(self, i):
        l = jnp.where((i >= CHUNKS) & (i < LAST), 1, 0)
        k, ci = lax.rem(i, 2), lax.rem(i, CHUNKS)
        hidden = rows_of(ci, CW)
        pairs = ((self.w_gate.at[l, :, hidden], self.wcg), (self.w_up.at[l, :, hidden], self.wcu), (self.w_down.at[l, hidden], self.wcd))
        return [pltpu.make_async_copy(src, dst.at[k], self.wsem.at[k, i]) for i, (src, dst) in enumerate(pairs)]

    def scale(self, h):
        return lax.rsqrt(jnp.mean(h * h, -1, keepdims=True) + 1e-6)

    def sweep(self, body, n=SUB, lo=0, hi=None):
        def step(t, carry):
            body(rows_of(t, n))
            return carry

        lax.fori_loop(lo, TOK // n if hi is None else hi, step, 0)

    def turn(self, src, dst):
        for i in EIGHT:
            for j in PAIR:
                dst[part(j, SUB), part(i, SUB)] = b16(dot_t(self.eye[...], src[part(i, SUB), part(j, SUB)]))

    def normed(self, rows, h):
        h = f32(h)
        self.a[rows] = b16(h * self.scale(h))

    def start(self):
        i, j = (lax.broadcasted_iota(jnp.int32, (SUB, SUB), axis) for axis in PAIR)
        self.eye[...] = b16(jnp.where(i == j, 1.0, 0.0))
        self.sweep(lambda rows: self.normed(rows, self.xv[rows]))

    def forward(self, i):
        k = lax.rem(i, 2)

        def body(rows):
            a = self.a[rows]
            for n in range(CW // SUB):
                cols = part(n, SUB)
                g = dot(a, self.wcg[k, :, cols])
                u = dot(a, self.wcu[k, :, cols])
                s = 0.5 * jnp.tanh(0.5 * g) + 0.5
                self.act[k, rows, cols] = b16(g * s * u)
            y = dot(self.act[k, rows], self.wcd[k])

            @pl.when(i == 0)
            def _():
                self.acc[rows] = y

            @pl.when(i > 0)
            def _():
                self.acc[rows] += y

        self.sweep(body, T)

    def layer_up(self):
        def body(rows):
            h = b16(f32(self.xv[rows]) + f32(b16(self.acc[rows])))
            self.h[rows] = h
            self.normed(rows, h)

        self.sweep(body)
        self.turn(self.a, self.at_)
        self.turn(self.dh, self.dht)

    def layer_down(self):
        def body(rows):
            h = f32(self.h[rows])
            s = self.scale(h)
            ct = f32(b16(self.acc[rows]))
            d = ct * s - h * (s * s * s * jnp.mean(ct * h, -1, keepdims=True))
            self.dh[rows] = b16(f32(self.dh[rows]) + f32(b16(d)))
            self.normed(rows, self.xv[rows])

        self.sweep(body)
        self.turn(self.a, self.at_)
        self.turn(self.dh, self.dht)

    def tiles(self, k, c, lo, hi):
        def body(rows):
            a, dh = self.a[rows], self.dh[rows]
            for n in range(CW // SUB):
                cols = part(n, SUB)
                g = dot(a, self.wcg[k, :, cols])
                u = dot(a, self.wcu[k, :, cols])
                d = f32(b16(dot_t(dh, self.wcd[k, cols])))
                s = 0.5 * jnp.tanh(0.5 * g) + 0.5
                sg = g * s
                self.act[k, rows, cols] = b16(sg * u)
                self.du[rows, cols] = b16(d * sg)
                self.dg[rows, cols] = b16(d * u * (s + sg * (1.0 - s)))

            @pl.when(c < CHUNKS)
            def _():
                v = dot_t(self.dg[rows], self.wcg[k]) + dot_t(self.du[rows], self.wcu[k])

                @pl.when(c == 0)
                def _():
                    self.acc[rows] = v

                @pl.when(c > 0)
                def _():
                    self.acc[rows] += v

        self.sweep(body, T, lo, hi)

    def save(self, i):
        return pltpu.make_async_copy(self.act.at[lax.rem(i, 2)], self.saved.at[i], self.asem.at[lax.rem(i, 2)])

    def load(self, c):
        return pltpu.make_async_copy(self.saved.at[c - CHUNKS], self.act.at[lax.rem(c, 2)], self.asem.at[lax.rem(c, 2)])

    def grads_down(self, c):
        k, kd = lax.rem(c, 2), lax.rem(c, 3)
        for n in range(CW // SUB):
            self.tmp[:, part(n, SUB)] = b16(dot(self.dht[...], self.act[k, :, part(n, SUB)]))
        for n in range(CW // SUB):
            v = dot_t(self.eye[...], self.tmp[:, part(n, SUB)])
            for i in range(SUB // 8):
                q, o = divmod(n * SUB + i * 8, 24)
                self.db[kd, q // 8, q % 8, o : o + 8, :] = b16(v[i * 8 : i * 8 + 8])

    def grads(self, k, n):
        cols = part(n, SUB)
        for src, dst in ((self.dg, self.gb), (self.du, self.ub)):
            dst[k, :, :, :, cols] = b16(dot(self.at_[...], src[:, cols])).reshape(*GU, SUB)


def vm(*shape, dtype=BF16):
    return pltpu.VMEM(shape, dtype)


GU = (4, 4, 32)
DN = (4, 8, 24, D)
SCRATCH = dict(
    xv=vm(TOK, D), h=vm(TOK, D), a=vm(TOK, D), at_=vm(D, TOK), dh=vm(TOK, D), dht=vm(D, TOK), acc=vm(TOK, D, dtype=F32),
    act=vm(2, TOK, CW), dg=vm(TOK, CW), du=vm(TOK, CW), eye=vm(SUB, SUB), tmp=vm(D, CW), wcg=vm(2, D, CW), wcu=vm(2, D, CW), wcd=vm(2, CW, D),
    gb=vm(2, *GU, CW), ub=vm(2, *GU, CW), db=vm(3, *DN),
    r1=vm(2, 2, 2, 2, 4, 32, HW), s2=vm(2, 2, 4, 32, HW), r2=vm(2, 2, 2, 4, 32, HW),
    s3=vm(2, 4, 2, 32, HW), r3=vm(2, 2, 3, 2, 32, HW), keep=vm(2, 2, 32, HW, dtype=F32),
    zf=vm(8, 2, 2, 4, HW, dtype=F32), zs=vm(8, 2, 2, 4, HW), zo=vm(2, 2, 4, HW, dtype=F32), fz=vm(7, 2, 2, 4, HW),
    nb=vm(2, 2, 4, HW), wz=vm(8, 2, 2, 4, HW), slabf=vm(2, 32, CW, dtype=F32), slab=vm(2, 32, CW),
    rz0=vm(2, 2, 4, 24, HD), rz=vm(2, 3, 2, 4, 24, D), sdy=vm(4, 24, D), rdy=vm(2, 3, 24, D), kdy=vm(24, D, dtype=F32),
    xb=vm(24, D), xo=vm(24, D, dtype=F32), fx=vm(2, 3, 24, D), nd=vm(24, D),
    ssem=pltpu.SemaphoreType.DMA((SEMS,)), rsem=pltpu.SemaphoreType.DMA((SEMS,)), lsem=pltpu.SemaphoreType.DMA((3,)),
    wsem=pltpu.SemaphoreType.DMA((2, 3)), xsem=pltpu.SemaphoreType.DMA((2,)), asem=pltpu.SemaphoreType.DMA((2,)),
)
HBM_IN = ("x_in", "dy", "w_gate", "w_up", "w_down")
VMEM_IN = ("wg", "wu", "wd", "mg", "mu", "md", "vg", "vu", "vd")
OUT = ("og", "ou", "od", "mog", "mou", "mod", "vog", "vou", "vod", "saved")

SLOTS = 9
EVENTS = dict(
    w1=(8, 8),
    w2=(12, 12),
    wi=(15, 16),
    wf=(19, 19),
    renew=(22, 25),
    gi=(27, 28),
    g1=(33, 37),
    g2=(40, 43),
    gend=(45, 51),
    d0=(5, 0),
    d1=(8, 3),
    d2=(12, 8),
    d3=(15, 12),
    dy_sum=(19, 17),
    dx=(23, 20),
    ex=(26, 24),
    ey=(29, 27),
    b0=(33, 31),
    b1=(38, 37),
    b2=(46, 46),
    b3=(53, 50),
    dend=(56, 58),
)
SPAN = max(p for both in EVENTS.values() for p in both) // SLOTS


def kernel(*refs):
    names = HBM_IN + VMEM_IN + OUT + tuple(SCRATCH)
    q = Step(dict(zip(names, refs, strict=True)))
    first = [pltpu.make_async_copy(src.at[0], dst, q.xsem.at[i]) for i, (src, dst) in enumerate(((q.x_in, q.xv), (q.dy, q.dh)))]
    go(first + q.weights(0))
    q.greet()
    first[0].wait()
    q.start()

    def forward(i, carry):
        go(q.weights(i + 1))
        for w in q.weights(i):
            w.wait()

        @pl.when(i >= 2)
        def _():
            q.save(i - 2).wait()

        run("forward", q.forward, i)
        q.save(i).start()
        return carry

    lax.fori_loop(0, CHUNKS, forward, 0)
    first[1].wait()
    run("layer_up", q.layer_up)
    for i in (CHUNKS - 2, CHUNKS - 1):
        q.save(i).wait()
    run("greeted", q.greeted)

    def chunk(c, carry):
        k = lax.rem(c, 2)

        @pl.when(c < LAST - 1)
        def _():
            go(q.weights(c + CHUNKS + 1))

        @pl.when((c >= CHUNKS - 1) & (c < LAST - 1))
        def _():
            q.load(c + 1).start()

        @pl.when(c < LAST)
        def _():
            for w in q.weights(c + CHUNKS):
                w.wait()

        @pl.when(c == CHUNKS)
        def _():
            run("layer_down", q.layer_down)

        def down():
            q.load(c).wait()
            q.grads_down(c)

        second, first_ = c < CHUNKS, (c >= CHUNKS) & (c < LAST)
        pieces = [(first_, down)] + [(c < LAST, lambda t=t: q.tiles(k, c, t, t + 1)) for t in FOUR] + [(second, lambda: q.grads_down(c))]
        pieces += [(c < LAST, lambda n=n: q.grads(k, n)) for n in range(CW // SUB)]
        for slot, (when, piece) in enumerate(pieces):

            @pl.when(when)
            def _():
                run("compute", piece)

            due = []
            for event, (second_at, first_at) in EVENTS.items():
                if second_at == first_at:
                    due.append((second_at, 0, LAST, event))
                else:
                    due += [(second_at, 0, CHUNKS, event), (first_at, CHUNKS, LAST, event)]
            for at, lo, hi, event in sorted(due, reverse=True):
                if at % SLOTS == slot:
                    back = at // SLOTS

                    @pl.when((c >= back + lo) & (c < back + hi))
                    def _():
                        run(event, getattr(q, event), c - back)

        return carry

    lax.fori_loop(0, LAST + SPAN, chunk, 0)


def run(name, f, *args):
    f(*args)


def solution(mesh):
    def local(x, dy, wg, wu, wd, *mv):
        d = lax.axis_index("dp")
        blocks = [lax.dynamic_slice_in_dim(w, d * n, n, 1) for w, n in ((wg, 4), (wu, 4), (wd, 24))]
        hbm, vmem = (pl.BlockSpec(memory_space=s) for s in (pl.ANY, pltpu.VMEM))
        news = [jax.ShapeDtypeStruct((2, *s), BF16) for s in ((*GU, FF), (*GU, FF), (4, *DN))]
        moments = [jax.ShapeDtypeStruct(t.shape, F32) for t in mv]
        out = pl.pallas_call(
            kernel,
            name="step",
            out_shape=news + moments + [jax.ShapeDtypeStruct((CHUNKS, TOK, CW), BF16)],
            in_specs=[hbm] * 5 + [vmem] * 9,
            out_specs=[hbm] * 3 + [vmem] * 6 + [hbm],
            scratch_shapes=list(SCRATCH.values()),
            compiler_params=pltpu.CompilerParams(collective_id=1, has_side_effects=True, vmem_limit_bytes=67043328),
        )(x, dy, wg, wu, wd, *blocks, *mv)
        return *(t.reshape(w.shape) for t, w in zip(out, (wg, wu, wd))), *out[3:-1]

    rows, whole = P(None, "dp", None), P()
    return jax.shard_map(
        local,
        mesh=mesh,
        in_specs=(P(("rep", "dp"), None, None),) * 2 + (whole,) * 3 + (rows,) * 6,
        out_specs=(P("rep", None, None),) * 3 + (P("rep", "dp", None),) * 6,
        check_vma=False,
    )
```

time: 317 us -> 262 us (0.83)
  Pallas kernels: 296 us -> 240 us
    pallas_call x1, Pallas kernels: 296 us -> 240 us  [local(): pl.pallas_call(kernel, name='step', out_shape=news + moments + [jax.Shape...]
where the time goes in v2:
time: 262 us
  Pallas kernels  240 us (92%)
  local copies, waits for them, and re-layouts  20.7 us (8%)
    pallas_call x1, Pallas kernels, local(): pl.pallas_call(kernel, name='step', out_shape=news + moments + [jax.Shape...  240 us
    unnamed x27, local copies, waits for them, and re-layouts  17.7 us

profile of v2, /device:TPU:2, one launch (start us, length us, event | category | flops | bytes accessed | tf_op | source)
XLA Modules:
  0.0 261.6 jit_solution(11027277731174252924)
XLA Ops:
  0.6 1.4 constant_dynamic-slice_fusion.refs_7_
  2.1 1.6 constant_dynamic-slice_fusion.1
  3.7 240.1 %step.1 = (bf16[2,4,4,32,3072]{4,3,2,1,0:T(8,128)(2,1)}, bf16[2,4,4,32,3072]{4,3,2,1,0:T(8,128)(2,1)}, bf16[2,4,4,8,24,512]{5,4,3,2,1,0:T(8,128)(2,1)}, f32[2,4,...) custom-call(bf16[1,2048,512]{2,1,0:T(8,128)(2,1)} %refs_0_.1, ...), custom_call_target="tpu_custom_call" | custom-call | tf_op jit(solution)/shard_map/step/pallas_call | solution.py:779
  243.8 0.0 copy-start
  243.8 0.0 slice-start
  243.8 6.6 %copy.29 = bf16[2,512,3072]{2,1,0:T(8,128)(2,1)} copy(bf16[2,512,3072]{2,1,0:T(8,128)(2,1)} %bitcast.7) | data formatting | bytes 12582912
  250.4 0.0 copy-done
  250.4 0.0 slice-start.1
  250.4 3.2 %copy.30 = bf16[2,512,3072]{2,1,0:T(8,128)(2,1)} copy(bf16[2,512,3072]{2,1,0:T(8,128)(2,1)S(1)} %bitcast.6) | data formatting | bytes 12582912
  253.6 0.0 slice-done
  253.6 1.3 slice-done.1
  255.0 0.0 copy-start.6
  255.0 0.0 copy-start.5
  255.0 0.0 copy-start.4
  255.0 0.0 copy-start.3
  255.0 0.0 copy-start.2
  255.0 0.0 copy-start.1
  255.0 2.7 %copy.31 = bf16[2,3072,512]{2,1,0:T(8,128)(2,1)} copy(bf16[2,3072,512]{2,1,0:T(8,128)(2,1)S(1)} %bitcast.5) | data formatting | bytes 12582912
  257.7 0.0 copy-done.6
  257.7 0.6 copy.32
  258.3 0.0 copy-done.5
  258.3 0.6 copy.33
  259.0 0.0 copy-done.4
  259.0 0.6 copy.34
  259.6 0.0 copy-done.3
  259.6 0.6 copy.35
  260.3 0.0 copy-done.2
  260.3 0.6 copy.36
  260.9 0.0 copy-done.1
  260.9 0.6 copy.37
  (1 shorter events, 0.0 us)
Async XLA Ops:
  243.8 6.6 %copy-start = (bf16[2,4,4,32,3072]{4,3,2,1,0:T(8,128)(2,1)S(1)}, bf16[2,4,4,32,3072]{4,3,2,1,0:T(8,128)(2,1)}, u32[]{:S(2)}) copy-start(bf16[2,4,4,32,3072]{4,3,2,1,0:T(8,128)(2,1)} %get-tuple-element.19) | copy-start | bytes 18874372
  243.8 9.8 %slice-start = ((s8[6291456]{0:T(1024)(128)(4,1)}), s8[4194304]{0:T(1024)(128)(4,1)S(1)}, s32[]{:S(2)}) async-start(s8[6291456]{0:T(1024)(128)(4,1)} %bitcast.3), calls=%async_computation | async-start | bytes 8388608
  250.4 4.5 %slice-start.1 = ((s8[6291456]{0:T(1024)(128)(4,1)}), s8[2097152]{0:T(1024)(128)(4,1)S(1)}, s32[]{:S(2)}) async-start(s8[6291456]{0:T(1024)(128)(4,1)} %bitcast.3), calls=%async_computation.1 | async-start | bytes 4194304
  255.0 2.7 %copy-start.6 = (f32[2,4,3072]{2,1,0:T(4,128)S(1)}, f32[2,4,3072]{2,1,0:T(4,128)}, u32[]{:S(2)}) copy-start(f32[2,4,3072]{2,1,0:T(4,128)} %get-tuple-element.41) | copy-start | bytes 294916
  255.0 3.4 %copy-start.5 = (f32[2,4,3072]{2,1,0:T(4,128)S(1)}, f32[2,4,3072]{2,1,0:T(4,128)}, u32[]{:S(2)}) copy-start(f32[2,4,3072]{2,1,0:T(4,128)} %get-tuple-element.42) | copy-start | bytes 294916
  255.0 4.0 %copy-start.4 = (f32[2,24,512]{2,1,0:T(8,128)S(1)}, f32[2,24,512]{2,1,0:T(8,128)}, u32[]{:S(2)}) copy-start(f32[2,24,512]{2,1,0:T(8,128)} %get-tuple-element.43) | copy-start | bytes 294916
  255.0 4.7 %copy-start.3 = (f32[2,4,3072]{2,1,0:T(4,128)S(1)}, f32[2,4,3072]{2,1,0:T(4,128)}, u32[]{:S(2)}) copy-start(f32[2,4,3072]{2,1,0:T(4,128)} %get-tuple-element.44) | copy-start | bytes 294916
  255.0 5.3 %copy-start.2 = (f32[2,4,3072]{2,1,0:T(4,128)S(1)}, f32[2,4,3072]{2,1,0:T(4,128)}, u32[]{:S(2)}) copy-start(f32[2,4,3072]{2,1,0:T(4,128)} %get-tuple-element.45) | copy-start | bytes 294916
  255.0 5.9 %copy-start.1 = (f32[2,24,512]{2,1,0:T(8,128)S(1)}, f32[2,24,512]{2,1,0:T(8,128)}, u32[]{:S(2)}) copy-start(f32[2,24,512]{2,1,0:T(8,128)} %get-tuple-element.46) | copy-start | bytes 294916

commit v3 on v2

--- a/solution.py
+++ b/solution.py
@@ -19,7 +19,9 @@
 FOUR = range(4)
 EIGHT = range(8)
 T = 512
+BIG = 1024
 SUB = 256
+VMEM_MAIN = 47300000
 
 
 def f32(v):
@@ -275,11 +277,9 @@
         for w in PAIR:
             for i in OTHERS:
                 j = self.up_inner(w, -i if get else i)
-                out.append((self.slab.at[w], self.orows(w, c, j if get else self.inner(w)), self.at_inner(w, j)))
+                ref = self.orows(w, c, j if get else self.inner(w))
+                out.append((ref, ref, self.at_inner(w, j)))
         return self.copies("a1", c, out)
-
-    def placed(self, c):
-        return [pltpu.make_async_copy(self.slab.at[w], self.orows(w, c, self.inner(w)), self.lsem.at[w]) for w in PAIR]
 
     def a3(self, c, get=False):
         out = []
@@ -299,17 +299,16 @@
 
     def gi(self, c):
         arrive(self.a0(c, True))
-        for w, h in self.halves():
-            for z in EIGHT:
-                self.slabf[w, 4 * z : 4 * z + 4, part(h, HW)] = f32(self.wz[z, w, h])
-        self.slab[...] = b16(self.slabf[...])
-        go(self.a1(c) + self.placed(c))
+        for w in PAIR:
+            for h in PAIR:
+                for z in EIGHT:
+                    self.slab[w, 4 * z : 4 * z + 4, part(h, HW)] = f32(self.wz[z, w, h])
+            self.orows(w, c, self.inner(w))[...] = b16(self.slab[w])
+        go(self.a1(c))
         leave(self.a0(c))
 
     def g1(self, c):
         arrive(self.a1(c, True))
-        for p in self.placed(c):
-            p.wait()
         go(self.a3(c))
         leave(self.a1(c))
 
@@ -417,10 +416,8 @@
         return self.od.at[layer_of(c), lax.rem(c, CHUNKS), y, self.z]
 
     def from_owner(self, c, i, x):
-        return self.copy(self.owner_sem("ex", c) + i, self.nd, self.dblock(c, self.y), self.at(x=x))
-
-    def placed_down(self, c):
-        return pltpu.make_async_copy(self.nd, self.dblock(c, self.y), self.lsem.at[2])
+        ref = self.dblock(c, self.y)
+        return self.copy(self.owner_sem("ex", c) + i, ref, ref, self.at(x=x))
 
     def dx(self, c):
         arrive(self.cy(c))
@@ -450,8 +447,7 @@
             for i in OTHERS:
                 self.to_owner(c, i, self.up_x(i)).wait_recv()
                 g = g + f32(self.fx[l, i - 1])
-            self.nd[...], self.mod[l], self.vod[l] = adamw(f32(self.wd[l]), self.md[l], self.vd[l], f32(b16(g)))
-            self.placed_down(c).start()
+            self.dblock(c, self.y)[...], self.mod[l], self.vod[l] = adamw(f32(self.wd[l]), self.md[l], self.vd[l], f32(b16(g)))
             for i in OTHERS:
                 self.from_owner(c, i, self.up_x(i)).start()
 
@@ -462,7 +458,6 @@
 
         @pl.when(self.away(c) == 0)
         def _():
-            self.placed_down(c).wait()
             for i in OTHERS:
                 self.from_owner(c, i, self.up_x(i)).wait_send()
 
@@ -535,36 +530,59 @@
     def start(self):
         i, j = (lax.broadcasted_iota(jnp.int32, (SUB, SUB), axis) for axis in PAIR)
         self.eye[...] = b16(jnp.where(i == j, 1.0, 0.0))
-        self.sweep(lambda rows: self.normed(rows, self.xv[rows]))
+        self.acc[...] = jnp.zeros_like(self.acc)
+
+    def start_rows(self):
+        self.sweep(lambda rows: self.normed(rows, self.xv[rows]), BIG)
+
+    def own_blocks(self):
+        tiles = [(l, w, j) for l in PAIR for w in PAIR for j in FOUR]
+        rows = rows_of(4 * self.x + self.y, 32)
+        refs = (self.w_gate, self.w_up)
+        out = [pltpu.make_async_copy(refs[w].at[l, rows, part(j, CW)], self.gb.at[l, w, j], self.osem.at[i]) for i, (l, w, j) in enumerate(tiles)]
+        mine = rows_of(32 * self.x + 8 * self.y + self.z, 24)
+        return out + [pltpu.make_async_copy(self.w_down.at[l, mine], self.wd.at[l], self.osem.at[len(tiles) + l]) for l in PAIR]
+
+    def pick_rows(self):
+        for l in PAIR:
+            for j in FOUR:
+                for w in PAIR:
+                    v = f32(self.gb[l, w, j])
+                    for z in EIGHT:
+                        for h in PAIR:
+                            self.zf[z, w, h] = v[4 * z : 4 * z + 4, h * HW : (h + 1) * HW]
+                    for h in PAIR:
+                        (self.wu if w else self.wg)[l, :, part(2 * j + h, HW)] = self.zf[self.z, w, h]
 
     def forward(self, i):
         k = lax.rem(i, 2)
 
-        def body(rows):
+        def tile(t, carry):
+            rows = rows_of(t, BIG)
+
+            @pl.when(i > 0)
+            def _():
+                self.save(i - 1, t).wait()
+
             a = self.a[rows]
             for n in range(CW // SUB):
                 cols = part(n, SUB)
                 g = dot(a, self.wcg[k, :, cols])
                 u = dot(a, self.wcu[k, :, cols])
                 s = 0.5 * jnp.tanh(0.5 * g) + 0.5
-                self.act[k, rows, cols] = b16(g * s * u)
-            y = dot(self.act[k, rows], self.wcd[k])
-
-            @pl.when(i == 0)
-            def _():
-                self.acc[rows] = y
-
-            @pl.when(i > 0)
-            def _():
-                self.acc[rows] += y
-
-        self.sweep(body, T)
+                self.act[rows, cols] = b16(g * s * u)
+            self.acc[rows] += dot(self.act[rows], self.wcd[k])
+            self.save(i, t).start()
+            return carry
+
+        lax.fori_loop(0, TOK // BIG, tile, 0)
 
     def layer_up(self):
         def body(rows):
             h = b16(f32(self.xv[rows]) + f32(b16(self.acc[rows])))
             self.h[rows] = h
             self.normed(rows, h)
+            self.acc[rows] = jnp.zeros((SUB, D), F32)
 
         self.sweep(body)
         self.turn(self.a, self.at_)
@@ -577,60 +595,57 @@
             ct = f32(b16(self.acc[rows]))
             d = ct * s - h * (s * s * s * jnp.mean(ct * h, -1, keepdims=True))
             self.dh[rows] = b16(f32(self.dh[rows]) + f32(b16(d)))
-            self.normed(rows, self.xv[rows])
 
         self.sweep(body)
+        self.kept_a().wait()
         self.turn(self.a, self.at_)
         self.turn(self.dh, self.dht)
 
-    def tiles(self, k, c, lo, hi):
+    def tiles(self, k, second, n, t):
         def body(rows):
             a, dh = self.a[rows], self.dh[rows]
-            for n in range(CW // SUB):
-                cols = part(n, SUB)
+            for i in range(CW // SUB):
+                cols = part(i, SUB)
                 g = dot(a, self.wcg[k, :, cols])
                 u = dot(a, self.wcu[k, :, cols])
                 d = f32(b16(dot_t(dh, self.wcd[k, cols])))
                 s = 0.5 * jnp.tanh(0.5 * g) + 0.5
                 sg = g * s
-                self.act[k, rows, cols] = b16(sg * u)
+                if second:
+                    self.act[rows, cols] = b16(sg * u)
                 self.du[rows, cols] = b16(d * sg)
                 self.dg[rows, cols] = b16(d * u * (s + sg * (1.0 - s)))
-
-            @pl.when(c < CHUNKS)
-            def _():
-                v = dot_t(self.dg[rows], self.wcg[k]) + dot_t(self.du[rows], self.wcu[k])
-
-                @pl.when(c == 0)
-                def _():
-                    self.acc[rows] = v
-
-                @pl.when(c > 0)
-                def _():
-                    self.acc[rows] += v
-
-        self.sweep(body, T, lo, hi)
-
-    def save(self, i):
-        return pltpu.make_async_copy(self.act.at[lax.rem(i, 2)], self.saved.at[i], self.asem.at[lax.rem(i, 2)])
+            if second:
+                self.acc[rows] += dot_t(self.dg[rows], self.wcg[k]) + dot_t(self.du[rows], self.wcu[k])
+
+        self.sweep(body, n, t, t + 1)
+
+    def save(self, i, t):
+        rows = rows_of(t, BIG)
+        return pltpu.make_async_copy(self.act.at[rows], self.saved.at[i, rows], self.asem.at[t])
 
     def load(self, c):
-        return pltpu.make_async_copy(self.saved.at[c - CHUNKS], self.act.at[lax.rem(c, 2)], self.asem.at[lax.rem(c, 2)])
+        return pltpu.make_async_copy(self.saved.at[c - CHUNKS], self.act, self.asem.at[0])
+
+    def keep_a(self):
+        return pltpu.make_async_copy(self.a, self.saved_a, self.asem.at[2])
+
+    def kept_a(self):
+        return pltpu.make_async_copy(self.saved_a, self.a, self.asem.at[2])
 
     def grads_down(self, c):
-        k, kd = lax.rem(c, 2), lax.rem(c, 3)
+        kd = lax.rem(c, 3)
         for n in range(CW // SUB):
-            self.tmp[:, part(n, SUB)] = b16(dot(self.dht[...], self.act[k, :, part(n, SUB)]))
+            self.tmp[:, part(n, SUB)] = b16(dot(self.dht[...], self.act[:, part(n, SUB)]))
         for n in range(CW // SUB):
             v = dot_t(self.eye[...], self.tmp[:, part(n, SUB)])
             for i in range(SUB // 8):
                 q, o = divmod(n * SUB + i * 8, 24)
                 self.db[kd, q // 8, q % 8, o : o + 8, :] = b16(v[i * 8 : i * 8 + 8])
 
-    def grads(self, k, n):
-        cols = part(n, SUB)
-        for src, dst in ((self.dg, self.gb), (self.du, self.ub)):
-            dst[k, :, :, :, cols] = b16(dot(self.at_[...], src[:, cols])).reshape(*GU, SUB)
+    def grads(self, k, w):
+        src, dst = (self.du, self.ub) if w else (self.dg, self.gb)
+        dst[k] = b16(dot(self.at_[...], src[...])).reshape(*GU, CW)
 
 
 def vm(*shape, dtype=BF16):
@@ -640,46 +655,46 @@
 GU = (4, 4, 32)
 DN = (4, 8, 24, D)
 SCRATCH = dict(
-    xv=vm(TOK, D), h=vm(TOK, D), a=vm(TOK, D), at_=vm(D, TOK), dh=vm(TOK, D), dht=vm(D, TOK), acc=vm(TOK, D, dtype=F32),
-    act=vm(2, TOK, CW), dg=vm(TOK, CW), du=vm(TOK, CW), eye=vm(SUB, SUB), tmp=vm(D, CW), wcg=vm(2, D, CW), wcu=vm(2, D, CW), wcd=vm(2, CW, D),
+    h=vm(TOK, D), a=vm(TOK, D), at_=vm(D, TOK), dh=vm(TOK, D), dht=vm(D, TOK), acc=vm(TOK, D, dtype=F32),
+    act=vm(TOK, CW), dg=vm(TOK, CW), du=vm(TOK, CW), eye=vm(SUB, SUB), tmp=vm(D, CW), wcg=vm(2, D, CW), wcu=vm(2, D, CW), wcd=vm(2, CW, D),
     gb=vm(2, *GU, CW), ub=vm(2, *GU, CW), db=vm(3, *DN),
     r1=vm(2, 2, 2, 2, 4, 32, HW), s2=vm(2, 2, 4, 32, HW), r2=vm(2, 2, 2, 4, 32, HW),
     s3=vm(2, 4, 2, 32, HW), r3=vm(2, 2, 3, 2, 32, HW), keep=vm(2, 2, 32, HW, dtype=F32),
     zf=vm(8, 2, 2, 4, HW, dtype=F32), zs=vm(8, 2, 2, 4, HW), zo=vm(2, 2, 4, HW, dtype=F32), fz=vm(7, 2, 2, 4, HW),
-    nb=vm(2, 2, 4, HW), wz=vm(8, 2, 2, 4, HW), slabf=vm(2, 32, CW, dtype=F32), slab=vm(2, 32, CW),
+    nb=vm(2, 2, 4, HW), wz=vm(8, 2, 2, 4, HW), slab=vm(2, 32, CW, dtype=F32),
     rz0=vm(2, 2, 4, 24, HD), rz=vm(2, 3, 2, 4, 24, D), sdy=vm(4, 24, D), rdy=vm(2, 3, 24, D), kdy=vm(24, D, dtype=F32),
-    xb=vm(24, D), xo=vm(24, D, dtype=F32), fx=vm(2, 3, 24, D), nd=vm(24, D),
-    ssem=pltpu.SemaphoreType.DMA((SEMS,)), rsem=pltpu.SemaphoreType.DMA((SEMS,)), lsem=pltpu.SemaphoreType.DMA((3,)),
-    wsem=pltpu.SemaphoreType.DMA((2, 3)), xsem=pltpu.SemaphoreType.DMA((2,)), asem=pltpu.SemaphoreType.DMA((2,)),
+    xb=vm(24, D), xo=vm(24, D, dtype=F32), fx=vm(2, 3, 24, D), wg=vm(2, 4, FF, dtype=F32), wu=vm(2, 4, FF, dtype=F32), wd=vm(2, 24, D),
+    ssem=pltpu.SemaphoreType.DMA((SEMS,)), rsem=pltpu.SemaphoreType.DMA((SEMS,)), osem=pltpu.SemaphoreType.DMA((18,)),
+    wsem=pltpu.SemaphoreType.DMA((2, 3)), xsem=pltpu.SemaphoreType.DMA((2,)), asem=pltpu.SemaphoreType.DMA((3,)),
 )
 HBM_IN = ("x_in", "dy", "w_gate", "w_up", "w_down")
-VMEM_IN = ("wg", "wu", "wd", "mg", "mu", "md", "vg", "vu", "vd")
-OUT = ("og", "ou", "od", "mog", "mou", "mod", "vog", "vou", "vod", "saved")
-
-SLOTS = 9
+VMEM_IN = ("mg", "mu", "md", "vg", "vu", "vd")
+OUT = ("og", "ou", "od", "mog", "mou", "mod", "vog", "vou", "vod", "saved", "saved_a")
+
+SLOTS = 8
 EVENTS = dict(
-    w1=(8, 8),
-    w2=(12, 12),
-    wi=(15, 16),
+    w1=(7, 7),
+    w2=(11, 11),
+    wi=(14, 14),
     wf=(19, 19),
-    renew=(22, 25),
-    gi=(27, 28),
-    g1=(33, 37),
-    g2=(40, 43),
-    gend=(45, 51),
+    renew=(23, 23),
+    gi=(27, 27),
+    g1=(32, 33),
+    g2=(37, 38),
+    gend=(42, 46),
     d0=(5, 0),
-    d1=(8, 3),
-    d2=(12, 8),
-    d3=(15, 12),
-    dy_sum=(19, 17),
-    dx=(23, 20),
-    ex=(26, 24),
-    ey=(29, 27),
-    b0=(33, 31),
-    b1=(38, 37),
-    b2=(46, 46),
-    b3=(53, 50),
-    dend=(56, 58),
+    d1=(7, 3),
+    d2=(11, 8),
+    d3=(14, 11),
+    dy_sum=(18, 15),
+    dx=(20, 18),
+    ex=(22, 21),
+    ey=(25, 24),
+    b0=(30, 28),
+    b1=(33, 32),
+    b2=(37, 37),
+    b3=(41, 42),
+    dend=(46, 47),
 )
 SPAN = max(p for both in EVENTS.values() for p in both) // SLOTS
 
@@ -687,30 +702,32 @@
 def kernel(*refs):
     names = HBM_IN + VMEM_IN + OUT + tuple(SCRATCH)
     q = Step(dict(zip(names, refs, strict=True)))
+    q.xv = q.dg.at[:, part(0, D)]
     first = [pltpu.make_async_copy(src.at[0], dst, q.xsem.at[i]) for i, (src, dst) in enumerate(((q.x_in, q.xv), (q.dy, q.dh)))]
-    go(first + q.weights(0))
+    go(first + q.weights(0) + q.own_blocks())
     q.greet()
+    run("start", q.start)
     first[0].wait()
-    q.start()
+    run("start_rows", q.start_rows)
+    q.keep_a().start()
 
     def forward(i, carry):
         go(q.weights(i + 1))
         for w in q.weights(i):
             w.wait()
 
-        @pl.when(i >= 2)
-        def _():
-            q.save(i - 2).wait()
-
         run("forward", q.forward, i)
-        q.save(i).start()
         return carry
 
     lax.fori_loop(0, CHUNKS, forward, 0)
     first[1].wait()
+    q.keep_a().wait()
     run("layer_up", q.layer_up)
-    for i in (CHUNKS - 2, CHUNKS - 1):
-        q.save(i).wait()
+    for t in PAIR:
+        q.save(CHUNKS - 1, t).wait()
+    for c in q.own_blocks():
+        c.wait()
+    run("pick_rows", q.pick_rows)
     run("greeted", q.greeted)
 
     def chunk(c, carry):
@@ -719,10 +736,6 @@
         @pl.when(c < LAST - 1)
         def _():
             go(q.weights(c + CHUNKS + 1))
-
-        @pl.when((c >= CHUNKS - 1) & (c < LAST - 1))
-        def _():
-            q.load(c + 1).start()
 
         @pl.when(c < LAST)
         def _():
@@ -737,14 +750,33 @@
             q.load(c).wait()
             q.grads_down(c)
 
-        second, first_ = c < CHUNKS, (c >= CHUNKS) & (c < LAST)
-        pieces = [(first_, down)] + [(c < LAST, lambda t=t: q.tiles(k, c, t, t + 1)) for t in FOUR] + [(second, lambda: q.grads_down(c))]
-        pieces += [(c < LAST, lambda n=n: q.grads(k, n)) for n in range(CW // SUB)]
-        for slot, (when, piece) in enumerate(pieces):
-
-            @pl.when(when)
+            @pl.when(c < LAST - 1)
             def _():
-                run("compute", piece)
+                q.load(c + 1).start()
+
+        def down_second():
+            q.grads_down(c)
+
+            @pl.when(c == CHUNKS - 1)
+            def _():
+                q.load(c + 1).start()
+                q.kept_a().start()
+
+        second, first_, both = c < CHUNKS, (c >= CHUNKS) & (c < LAST), c < LAST
+        pieces = {slot: [] for slot in range(SLOTS)}
+        pieces[0].append((first_, down))
+        for t in FOUR:
+            pieces[1 + t].append((second, lambda t=t: q.tiles(k, True, T, t)))
+        for t in PAIR:
+            pieces[2 + 2 * t].append((first_, lambda t=t: q.tiles(k, False, BIG, t)))
+            pieces[6 + t].append((both, lambda t=t: q.grads(k, t)))
+        pieces[5].append((second, down_second))
+        for slot in range(SLOTS):
+            for when, piece in pieces[slot]:
+
+                @pl.when(when)
+                def _():
+                    run("compute", piece)
 
             due = []
             for event, (second_at, first_at) in EVENTS.items():
@@ -769,23 +801,39 @@
     f(*args)
 
 
+def place(*refs):
+    n = len(refs) // 2
+    copies = [pltpu.make_async_copy(src, dst, refs[-1].at[i]) for i, (src, dst) in enumerate(zip(refs[:n], refs[n:-1], strict=True))]
+    go(copies)
+    for c in copies:
+        c.wait()
+
+
 def solution(mesh):
     def local(x, dy, wg, wu, wd, *mv):
-        d = lax.axis_index("dp")
-        blocks = [lax.dynamic_slice_in_dim(w, d * n, n, 1) for w, n in ((wg, 4), (wu, 4), (wd, 24))]
         hbm, vmem = (pl.BlockSpec(memory_space=s) for s in (pl.ANY, pltpu.VMEM))
         news = [jax.ShapeDtypeStruct((2, *s), BF16) for s in ((*GU, FF), (*GU, FF), (4, *DN))]
         moments = [jax.ShapeDtypeStruct(t.shape, F32) for t in mv]
+        kept = [jax.ShapeDtypeStruct(s, BF16) for s in ((CHUNKS, TOK, CW), (TOK, D))]
         out = pl.pallas_call(
             kernel,
             name="step",
-            out_shape=news + moments + [jax.ShapeDtypeStruct((CHUNKS, TOK, CW), BF16)],
-            in_specs=[hbm] * 5 + [vmem] * 9,
-            out_specs=[hbm] * 3 + [vmem] * 6 + [hbm],
+            out_shape=[pltpu.VMEM(t.shape, t.dtype) for t in news + moments] + kept,
+            in_specs=[hbm] * 5 + [vmem] * 6,
+            out_specs=[vmem] * 9 + [hbm] * 2,
             scratch_shapes=list(SCRATCH.values()),
-            compiler_params=pltpu.CompilerParams(collective_id=1, has_side_effects=True, vmem_limit_bytes=67043328),
-        )(x, dy, wg, wu, wd, *blocks, *mv)
-        return *(t.reshape(w.shape) for t, w in zip(out, (wg, wu, wd))), *out[3:-1]
+            compiler_params=pltpu.CompilerParams(collective_id=1, has_side_effects=True, vmem_limit_bytes=VMEM_MAIN),
+        )(x, dy, wg, wu, wd, *mv)
+        placed = pl.pallas_call(
+            place,
+            name="place",
+            out_shape=news + moments,
+            in_specs=[vmem] * 9,
+            out_specs=[hbm] * 9,
+            scratch_shapes=[pltpu.SemaphoreType.DMA((9,))],
+            compiler_params=pltpu.CompilerParams(vmem_limit_bytes=1 << 20),
+        )(*out[:9])
+        return *(t.reshape(w.shape) for t, w in zip(placed, (wg, wu, wd))), *placed[3:]
 
     rows, whole = P(None, "dp", None), P()
     return jax.shard_map(

time: 262 us -> 240 us (0.916)
  local copies, waits for them, and re-layouts: 20.7 us -> 0 us
    unnamed x27 -> x0, local copies, waits for them, and re-layouts: 17.7 us -> none
    dynamic_slice x2 -> x0, local copies, waits for them, and re-layouts: 3.06 us -> none  [local(): lax.dynamic_slice_in_dim(w, d * n, n, 1)]
    pallas_call x1 -> x2, Pallas kernels: 240 us -> 240 us  [the longest x1 233 us: local(): pl.pallas_call(kernel, name='step', out_shape=[pltpu.VMEM(t.shape, t.dtyp...]
where the time goes in v3:
time: 240 us
  Pallas kernels  240 us (100%)
    pallas_call x1, Pallas kernels, local(): pl.pallas_call(kernel, name='step', out_shape=[pltpu.VMEM(t.shape, t.dtyp...  233 us
    pallas_call x1, Pallas kernels, local(): pl.pallas_call(place, name='place', out_shape=news + moments, in_specs=[v...  6.76 us

profile of v3, /device:TPU:2, one launch (start us, length us, event | category | flops | bytes accessed | tf_op | source)
XLA Modules:
  0.0 240.4 jit_solution(14953935666203855099)
XLA Ops:
  0.6 232.8 %step.1 = (bf16[2,4,4,32,3072]{4,3,2,1,0:T(8,128)(2,1)S(1)}, bf16[2,4,4,32,3072]{4,3,2,1,0:T(8,128)(2,1)S(1)}, bf16[2,4,4,8,24,512]{5,4,3,2,1,0:T(8,128)(2,1)S(1...) custom-call(bf16[1,2048,512]{2,1,0:T(8,128)(2,1)} %refs_0_.1, ...), custom_call_target="tpu_custom_call" | custom-call | tf_op jit(solution)/shard_map/step/pallas_call | solution.py:818
  233.4 6.8 %place.1 = (bf16[2,4,4,32,3072]{4,3,2,1,0:T(8,128)(2,1)}, bf16[2,4,4,32,3072]{4,3,2,1,0:T(8,128)(2,1)}, bf16[2,4,4,8,24,512]{5,4,3,2,1,0:T(8,128)(2,1)}, f32[2,4...) custom-call(bf16[2,4,4,32,3072]{4,3,2,1,0:T(8,128)(2,1)S(1)} %get-tu, ...), custom_call_target="tpu_custom_call" | custom-call | tf_op jit(solution)/shard_map/place/pallas_call | solution.py:827

commit v4 on v3

--- a/solution.py
+++ b/solution.py
@@ -582,9 +582,9 @@
             h = b16(f32(self.xv[rows]) + f32(b16(self.acc[rows])))
             self.h[rows] = h
             self.normed(rows, h)
-            self.acc[rows] = jnp.zeros((SUB, D), F32)
-
-        self.sweep(body)
+            self.acc[rows] = jnp.zeros((BIG, D), F32)
+
+        self.sweep(body, BIG)
         self.turn(self.a, self.at_)
         self.turn(self.dh, self.dht)
 
@@ -596,7 +596,7 @@
             d = ct * s - h * (s * s * s * jnp.mean(ct * h, -1, keepdims=True))
             self.dh[rows] = b16(f32(self.dh[rows]) + f32(b16(d)))
 
-        self.sweep(body)
+        self.sweep(body, BIG)
         self.kept_a().wait()
         self.turn(self.a, self.at_)
         self.turn(self.dh, self.dht)
@@ -677,24 +677,24 @@
     w2=(11, 11),
     wi=(14, 14),
     wf=(19, 19),
-    renew=(23, 23),
+    renew=(23, 22),
     gi=(27, 27),
-    g1=(32, 33),
-    g2=(37, 38),
-    gend=(42, 46),
+    g1=(32, 35),
+    g2=(37, 42),
+    gend=(40, 50),
     d0=(5, 0),
     d1=(7, 3),
-    d2=(11, 8),
+    d2=(11, 7),
     d3=(14, 11),
     dy_sum=(18, 15),
     dx=(20, 18),
     ex=(22, 21),
     ey=(25, 24),
     b0=(30, 28),
-    b1=(33, 32),
-    b2=(37, 37),
-    b3=(41, 42),
-    dend=(46, 47),
+    b1=(33, 34),
+    b2=(41, 41),
+    b3=(44, 46),
+    dend=(52, 54),
 )
 SPAN = max(p for both in EVENTS.values() for p in both) // SLOTS
 
@@ -704,12 +704,12 @@
     q = Step(dict(zip(names, refs, strict=True)))
     q.xv = q.dg.at[:, part(0, D)]
     first = [pltpu.make_async_copy(src.at[0], dst, q.xsem.at[i]) for i, (src, dst) in enumerate(((q.x_in, q.xv), (q.dy, q.dh)))]
-    go(first + q.weights(0) + q.own_blocks())
+    go(first[:1] + q.weights(0))
     q.greet()
     run("start", q.start)
     first[0].wait()
     run("start_rows", q.start_rows)
-    q.keep_a().start()
+    go(first[1:] + [q.keep_a()] + q.own_blocks())
 
     def forward(i, carry):
         go(q.weights(i + 1))

time: 240 us -> 238 us (level)
  Pallas kernels: 240 us -> 237 us
where the time goes in v4:
time: 238 us
  Pallas kernels  237 us (100%)
    pallas_call x1, Pallas kernels, local(): pl.pallas_call(kernel, name='step', out_shape=[pltpu.VMEM(t.shape, t.dtyp...  230 us
    pallas_call x1, Pallas kernels, local(): pl.pallas_call(place, name='place', out_shape=news + moments, in_specs=[v...  6.76 us

profile of v4, /device:TPU:2, one launch (start us, length us, event | category | flops | bytes accessed | tf_op | source)
XLA Modules:
  0.0 238.0 jit_solution(9003741529406368686)
XLA Ops:
  0.6 230.4 %step.1 = (bf16[2,4,4,32,3072]{4,3,2,1,0:T(8,128)(2,1)S(1)}, bf16[2,4,4,32,3072]{4,3,2,1,0:T(8,128)(2,1)S(1)}, bf16[2,4,4,8,24,512]{5,4,3,2,1,0:T(8,128)(2,1)S(1...) custom-call(bf16[1,2048,512]{2,1,0:T(8,128)(2,1)} %refs_0_.1, ...), custom_call_target="tpu_custom_call" | custom-call | tf_op jit(solution)/shard_map/step/pallas_call | solution.py:818
  231.1 6.8 %place.1 = (bf16[2,4,4,32,3072]{4,3,2,1,0:T(8,128)(2,1)}, bf16[2,4,4,32,3072]{4,3,2,1,0:T(8,128)(2,1)}, bf16[2,4,4,8,24,512]{5,4,3,2,1,0:T(8,128)(2,1)}, f32[2,4...) custom-call(bf16[2,4,4,32,3072]{4,3,2,1,0:T(8,128)(2,1)S(1)} %get-tu, ...), custom_call_target="tpu_custom_call" | custom-call | tf_op jit(solution)/shard_map/place/pallas_call | solution.py:827

commit v5 on v4

--- a/solution.py
+++ b/solution.py
@@ -681,20 +681,20 @@
     gi=(27, 27),
     g1=(32, 35),
     g2=(37, 42),
-    gend=(40, 50),
+    gend=(43, 46),
     d0=(5, 0),
     d1=(7, 3),
     d2=(11, 7),
     d3=(14, 11),
     dy_sum=(18, 15),
     dx=(20, 18),
-    ex=(22, 21),
+    ex=(22, 20),
     ey=(25, 24),
     b0=(30, 28),
     b1=(33, 34),
     b2=(41, 41),
-    b3=(44, 46),
-    dend=(52, 54),
+    b3=(44, 45),
+    dend=(49, 53),
 )
 SPAN = max(p for both in EVENTS.values() for p in both) // SLOTS
 
@@ -803,7 +803,8 @@
 
 def place(*refs):
     n = len(refs) // 2
-    copies = [pltpu.make_async_copy(src, dst, refs[-1].at[i]) for i, (src, dst) in enumerate(zip(refs[:n], refs[n:-1], strict=True))]
+    pairs = list(zip(refs[:n], refs[n:-1], strict=True))
+    copies = [pltpu.make_async_copy(src.at[l], dst.at[l], refs[-1].at[i, l]) for i, (src, dst) in enumerate(pairs) for l in PAIR]
     go(copies)
     for c in copies:
         c.wait()
@@ -830,7 +831,7 @@
             out_shape=news + moments,
             in_specs=[vmem] * 9,
             out_specs=[hbm] * 9,
-            scratch_shapes=[pltpu.SemaphoreType.DMA((9,))],
+            scratch_shapes=[pltpu.SemaphoreType.DMA((9, 2))],
             compiler_params=pltpu.CompilerParams(vmem_limit_bytes=1 << 20),
         )(*out[:9])
         return *(t.reshape(w.shape) for t, w in zip(placed, (wg, wu, wd))), *placed[3:]

time: 238 us -> 239 us (level)
  no operation moved by 1% of the time
where the time goes in v5:
time: 239 us
  Pallas kernels  238 us (100%)
    pallas_call x1, Pallas kernels, local(): pl.pallas_call(kernel, name='step', out_shape=[pltpu.VMEM(t.shape, t.dtyp...  231 us
    pallas_call x1, Pallas kernels, local(): pl.pallas_call(place, name='place', out_shape=news + moments, in_specs=[v...  6.81 us

profile of v5, /device:TPU:2, one launch (start us, length us, event | category | flops | bytes accessed | tf_op | source)
XLA Modules:
  0.0 238.9 jit_solution(12982163187461103591)
XLA Ops:
  0.6 231.2 %step.1 = (bf16[2,4,4,32,3072]{4,3,2,1,0:T(8,128)(2,1)S(1)}, bf16[2,4,4,32,3072]{4,3,2,1,0:T(8,128)(2,1)S(1)}, bf16[2,4,4,8,24,512]{5,4,3,2,1,0:T(8,128)(2,1)S(1...) custom-call(bf16[1,2048,512]{2,1,0:T(8,128)(2,1)} %refs_0_.1, ...), custom_call_target="tpu_custom_call" | custom-call | tf_op jit(solution)/shard_map/step/pallas_call | solution.py:819
  231.9 6.8 %place.1 = (bf16[2,4,4,32,3072]{4,3,2,1,0:T(8,128)(2,1)}, bf16[2,4,4,32,3072]{4,3,2,1,0:T(8,128)(2,1)}, bf16[2,4,4,8,24,512]{5,4,3,2,1,0:T(8,128)(2,1)}, f32[2,4...) custom-call(bf16[2,4,4,32,3072]{4,3,2,1,0:T(8,128)(2,1)S(1)} %get-tu, ...), custom_call_target="tpu_custom_call" | custom-call | tf_op jit(solution)/shard_map/place/pallas_call | solution.py:828
